TPU v7x, 32 devices: a whole 2x2x4 slice. The times are simulated.
32 devices in a mesh: row: 4 (over y, x), col: 8 (over z, core).
Axes of the slice: x: 2, y: 2, z: 4, core: 2. Of those that a mesh axis runs over, the one named last changes fastest.
Arguments:
- object_tiles: float32 [2, 2, 1024, 2048], P(None, None, 'row', 'col'), may hold values from -4 to 4
- probe: float32 [2, 256, 256], replicated, may hold values from -5 to 5
- phase: float32 [256, 256], replicated, may hold values from -3.140625 to 3.140625
- measured: float32 [64, 256, 256], P(('row', 'col')), may hold values from 0 to 2
- offsets: int32 [64, 2], P(('row', 'col')), may hold values from 0 to 256
- live: int32 [4, 8], P('row', 'col'), may hold values from 1 to 2, as said below
Outputs:
- object_next: float32 [2, 2, 1024, 2048], P(None, None, 'row', 'col')
- object_grad: float32 [2, 2, 1024, 2048], P(None, None, 'row', 'col')
Inputs may be any that keep to these rules, and one draw needn't show every extreme that they name: `live`: every tile has at least one used slot, and some tile uses all 2; used slots come first.
All inputs are finite; a program needn't handle non-finite values.
Results may differ from a plain program's by a relative error of at most 0.0003.
Values sent between devices are 32-bit elements; how exact they have to be, the bound alone decides.
No kernel may reach another device: no remote copies, remote signals or barrier semaphores. Data moves between devices by JAX's collectives and lax.ppermute only.
A program may use at most 64 MiB of HBM per device.

v0:
```python
import functools
import math

import jax
import jax.numpy as jnp
import numpy as np
from jax import lax
from jax.experimental import pallas as pl
from jax.experimental.pallas import tpu as pltpu
from jax.sharding import PartitionSpec as P


step_size = 0.5


F32 = jnp.float32
BF16 = jnp.bfloat16
VMEM = pl.BlockSpec(memory_space=pltpu.VMEM)
SMEM = pl.BlockSpec(memory_space=pltpu.SMEM)
ANY = pl.BlockSpec(memory_space=pl.ANY)


def split(value):
    high = value.astype(BF16)
    return high, (value - high.astype(F32)).astype(BF16)


def dft_table(length):
    index = np.arange(length)
    angles = (index[:, None] * index[None, :] % length) * (2.0 * math.pi / length)
    cosine, sine = (np.cos(angles) / math.sqrt(length), np.sin(angles) / math.sqrt(length))
    table = np.stack([cosine, cosine + sine, cosine - sine])
    high = table.astype(np.float32).astype(BF16)
    low = (table - high.astype(np.float64)).astype(np.float32).astype(BF16)
    return np.stack([high, low])


def spread(high, low, place, a, b):
    for form, value in enumerate((a + b, a, b)):
        high[(form, *place)], low[(form, *place)] = split(value)


def join(one, two, three):
    return one - three, one - two


def transform(conj, load, store, table, scratch):
    xh, xl, zh, zl = scratch
    length = xh.shape[1]
    slots = xh.shape[2] // length
    order = (1, 0) if conj else (0, 1)
    for slot in range(slots):
        parts = load(slot)
        cols = pl.ds(slot * length, length)
        spread(xh, xl, (slice(None), cols), parts[order[0]], parts[order[1]])
    products = []
    for form in range(3):
        lhs = jnp.concatenate([table[0, form], table[1, form], table[0, form]], axis=1)
        rhs = jnp.concatenate([xh[form], xh[form], xl[form]], axis=0)
        products.append(jnp.dot(lhs, rhs, preferred_element_type=F32))
    z = join(*products)
    for slot in range(slots):
        at = slice(slot * length, (slot + 1) * length)
        spread(zh, zl, (pl.ds(slot * length, length), slice(None)), z[0][:, at], z[1][:, at])
    for slot in range(slots):
        rows = pl.ds(slot * length, length)
        products = []
        for form in range(3):
            lhs = jnp.concatenate([zh[form, rows], zl[form, rows], zh[form, rows]], axis=1)
            rhs = jnp.concatenate([table[0, form], table[0, form], table[1, form]], axis=0)
            products.append(jnp.dot(lhs, rhs, preferred_element_type=F32))
        both = join(*products)
        store(slot, both[order[0]], both[order[1]])


def gather_slice(which, pieces, ext):
    tile, rows, sides, corners = pieces[0], pieces[1:3], pieces[3:5], pieces[5:7]
    margin = rows[0].shape[1]
    places = places_of(margin, *tile.shape[2:])
    inner_rows, inner_cols = pl.ds(margin, tile.shape[2]), pl.ds(margin, tile.shape[3])
    outer_rows, outer_cols = halves(places, 0, margin), halves(places, 2, margin)
    for part in range(2):
        ext[part, inner_rows, inner_cols] = tile[which, part]
        for k in range(2):
            ext[part, outer_rows[k], inner_cols] = rows[k][part]
            ext[part, inner_rows, outer_cols[k]] = sides[k][which, part]
            for j in range(2):
                ext[part, outer_rows[j], outer_cols[k]] = corners[k][j, part]


def places_of(margin, high, wide):
    row_at, col_at = lax.axis_index("row"), lax.axis_index("col")
    last = lax.axis_size("row") - 1
    row_e = jnp.where(row_at % 2 == 0, margin + high, 0)
    col_e = jnp.where(col_at % 2 == 0, margin + wide, 0)
    partnered = (row_at > 0) & ((row_at < last) | (last % 2 == 0))
    return row_e, margin + high - row_e, col_e, margin + wide - col_e, partnered


def halves(places, first, margin):
    return [pl.ds(pl.multiple_of(places[first + k], 128), margin) for k in range(2)]


def inner_halves(places, first, margin):
    at = [jnp.maximum(places[first + k] - 2 * margin, 0) for k in range(2)]
    return [pl.ds(pl.multiple_of(start, 128), margin) for start in at]


def hand_out(gext, corners, sides, middle):
    margin = corners[0].shape[2]
    places = places_of(margin, sides[0].shape[1], middle.shape[2])
    inner_rows, inner_cols = pl.ds(margin, sides[0].shape[1]), pl.ds(margin, middle.shape[2])
    outer_rows, outer_cols = halves(places, 0, margin), halves(places, 2, margin)
    for part in range(2):
        for k in range(2):
            for j in range(2):
                corners[k][j, part] = gext[part, outer_rows[j], outer_cols[k]]
            sides[k][part] = gext[part, inner_rows, outer_cols[k]]
        middle[part] = gext[part, :, inner_cols]


def place(slots_at, slot, shape, length):
    spans, shifts = ([], [])
    for axis, tile in ((0, 8), (1, 128)):
        at = slots_at[2 * slot + axis]
        base = jnp.minimum(at // tile, (shape[axis + 1] - length) // tile - 1)
        spans.append(pl.ds(pl.multiple_of(base * tile, tile), length + tile))
        shifts.append(at - base * tile)
    return spans, shifts


def window(ext, slots_at, slot, length):
    (rows, cols), (down, along) = place(slots_at, slot, ext.shape, length)
    groups = length // 8
    sublane = lax.broadcasted_iota(jnp.int32, (1, 8, 1), 1) < 8 - down
    lane = lax.broadcasted_iota(jnp.int32, (1, 128), 1) < 128 - along
    parts = []
    for part in range(2):
        tall = ext[part, rows, cols].reshape(groups + 1, 8, length + 128)
        tall = pltpu.roll(tall, lax.rem(8 - down, 8), axis=1)
        flat = jnp.where(sublane, tall[:-1], tall[1:]).reshape(length, length + 128)
        turned = [
            pltpu.roll(flat[:, at : at + 128], lax.rem(128 - along, 128), axis=1)
            for at in range(0, length + 128, 128)
        ]
        pieces = [jnp.where(lane, *pair) for pair in zip(turned[:-1], turned[1:])]
        parts.append(jnp.concatenate(pieces, axis=1))
    return parts


def scatter(gext, slots_at, slot, grads):
    length = grads[0].shape[0]
    (rows, cols), (down, along) = place(slots_at, slot, gext.shape, length)
    groups = length // 8
    sublane = lax.broadcasted_iota(jnp.int32, (1, 8, 1), 1) >= down
    lane = lax.broadcasted_iota(jnp.int32, (1, 128), 1) >= along
    for part in range(2):
        turned = [
            pltpu.roll(grads[part][:, at : at + 128], lax.rem(along, 128), axis=1)
            for at in range(0, length, 128)
        ]
        none = jnp.zeros((length, 128), F32)
        pieces = [jnp.where(lane, *pair) for pair in zip([*turned, none], [none, *turned])]
        flat = jnp.concatenate(pieces, axis=1).reshape(groups, 8, length + 128)
        flat = pltpu.roll(flat, lax.rem(down, 8), axis=1)
        none = jnp.zeros((1, 8, length + 128), F32)
        after, before = (jnp.concatenate(pair, axis=0) for pair in ((flat, none), (none, flat)))
        tall = jnp.where(sublane, after, before).reshape(length + 8, length + 128)
        gext[part, rows, cols] += tall


def multiply(a, b):
    return a[0] * b[0] - a[1] * b[1], a[0] * b[1] + a[1] * b[0]


def multiply_conj(a, b):
    return a[0] * b[0] + a[1] * b[1], a[0] * b[1] - a[1] * b[0]


def put(ref, slot, re, im):
    ref[0, slot] = re
    ref[1, slot] = im


def near_kernel(
    slots_at, tile, row_e, row_o, side_e, side_o, corner_e, corner_o, probe, kernel, left, near,
    ext, mid, xh, xl, zh, zl,
):
    scratch = (xh, xl, zh, zl)
    length = probe.shape[1]
    pieces = (tile, row_e, row_o, side_e, side_o, corner_e, corner_o)
    gather_slice(0, pieces, ext)

    def first(slot):
        return multiply(probe, window(ext, slots_at, slot, length))

    def moved(slot, re, im):
        put(mid, slot, *multiply((re, im), kernel))

    transform(False, first, moved, left, scratch)
    transform(
        True, lambda slot: (mid[0, slot], mid[1, slot]), functools.partial(put, near),
        left, scratch,
    )


def exit_kernel(
    slots_at, tile, row_e, row_o, side_e, side_o, corner_e, corner_o, near, measured, left,
    g_near, out_ce, out_co, out_se, out_so, middle, gext, ext, mid, cut, xh, xl,
    zh, zl,
):
    scratch = (xh, xl, zh, zl)
    length = near.shape[2]
    pieces = (tile, row_e, row_o, side_e, side_o, corner_e, corner_o)
    gather_slice(1, pieces, ext)
    gext[...] = jnp.zeros(gext.shape, F32)

    def exiting(slot):
        put(cut, slot, *window(ext, slots_at, slot, length))
        return multiply((near[0, slot], near[1, slot]), (cut[0, slot], cut[1, slot]))

    def residual(slot, re, im):
        weight = jnp.where(slot < slots_at[2 * near.shape[1]], 1.0, 0.0).astype(F32)
        factor = weight * (re * re + im * im - measured[slot])
        put(mid, slot, factor * re, factor * im)

    def back(slot, re, im):
        put(g_near, slot, *multiply_conj((cut[0, slot], cut[1, slot]), (re, im)))
        scatter(gext, slots_at, slot, multiply_conj((near[0, slot], near[1, slot]), (re, im)))

    transform(False, exiting, residual, left, scratch)
    transform(True, lambda slot: (mid[0, slot], mid[1, slot]), back, left, scratch)
    hand_out(gext, (out_ce, out_co), (out_se, out_so), middle)


def first_kernel(
    slots_at, g_near, probe, kernel, left, one_se, one_so, out_ce, out_co, out_se,
    out_so, middle, gext, mid, xh, xl, zh, zl,
):
    scratch = (xh, xl, zh, zl)
    gext[...] = jnp.zeros(gext.shape, F32)

    def moved(slot, re, im):
        put(mid, slot, *multiply_conj(kernel, (re, im)))

    def back(slot, re, im):
        scatter(gext, slots_at, slot, multiply_conj(probe, (re, im)))

    transform(
        False, lambda slot: (g_near[0, slot], g_near[1, slot]), moved, left, scratch
    )
    transform(True, lambda slot: (mid[0, slot], mid[1, slot]), back, left, scratch)
    hand_out(gext, (out_ce, out_co), (out_se.at[0], out_so.at[0]), middle)
    out_se[1] = one_se[...]
    out_so[1] = one_so[...]


def corner_kernel(middle, corner_e, corner_o, strip_e, *strips_o):
    corners, margin = (corner_e, corner_o), corner_e.shape[2]
    places = places_of(margin, middle.shape[1] - 2 * margin, middle.shape[2])
    rows, cols = halves(places, 0, margin), inner_halves(places, 2, margin)
    for part in range(2):
        for strip, at in ((strip_e.at[part], rows[0]), (half(strips_o, part), rows[1])):
            strip[...] = middle[part, at, :]
            for k in range(2):
                strip[:, cols[k]] += corners[k][int(at is rows[1]), part]
    if len(strips_o) == 2:
        relayed = strips_o[1]
        relayed[...] = jnp.where(places[4], relayed[...], 0.0)


def half(strips, part):
    return strips[part].at[0] if len(strips) == 2 else strips[0].at[part]


def final_kernel(steps, tile, side_e, side_o, *refs):
    after, grad, new_after, new_grad, sems = refs[-5:]
    margin = side_e.shape[3]
    places = places_of(margin, *tile.shape[2:])
    rows, cols = inner_halves(places, 0, margin), inner_halves(places, 2, margin)
    copies = []
    for index, (which, side, middle, arrived) in enumerate(steps):
        arrived = [refs[at] for at in arrived]
        outer = pl.ds(pl.multiple_of(rows[side].start + margin, 128), margin)
        for part in range(2):
            new = new_grad.at[index, part]
            new[...] = refs[middle][part, outer, :] + half(arrived, part)[...]
            for k in range(2):
                new[:, cols[k]] += (side_e, side_o)[k][which, part, rows[side], :]
            stepped = tile[which, part, rows[side], :] - step_size * new[...]
            new_after[index, part] = stepped
            for at, (source, out) in enumerate(((new_after, after), (new_grad, grad))):
                copy = pltpu.make_async_copy(
                    source.at[index, part], out.at[which, part, rows[side], :],
                    sems.at[index, part, at],
                )
                copy.start()
                copies.append(copy)
    for copy in copies:
        copy.wait()


def edge_kernel(tile, row_e0, row_o0, row_e1, row_o1, side_e, side_o):
    margin = row_e0.shape[1]
    places = places_of(margin, *tile.shape[2:])
    rows, cols = inner_halves(places, 0, margin), inner_halves(places, 2, margin)
    for which, outs in enumerate(((row_e0, row_o0), (row_e1, row_o1))):
        for part in range(2):
            for k in range(2):
                outs[k][part] = tile[which, part, rows[k], :]
                (side_e, side_o)[k][which, part] = tile[which, part, :, cols[k]]
    row_o1[...] = jnp.where(places[4], row_o1[...], 0.0)


def cut_kernel(halo_e, halo_o, to_even, to_odd):
    margin = to_even.shape[2]
    cols = inner_halves(places_of(margin, 0, halo_e.shape[2]), 2, margin)
    for j, halo in enumerate((halo_e, halo_o)):
        for part in range(2):
            to_even[j, part] = halo[part, :, cols[0]]
            to_odd[j, part] = halo[part, :, cols[1]]


def turn_kernel(offsets, live, phase, table, light, slots_at, kernel, left, probe):
    for slot in range(offsets.shape[0]):
        for axis in range(2):
            slots_at[2 * slot + axis] = offsets[slot, axis]
    slots_at[2 * offsets.shape[0]] = live[0, 0]
    left[...] = table[...]
    probe[...] = light[...]
    kernel[0] = jnp.cos(phase[...])
    kernel[1] = jnp.sin(phase[...])


def even_pairs(count):
    return [(low, low + 1) for low in range(0, count - 1, 2)]


def odd_pairs(count):
    return [(low, low + 1) for low in range(1, count - 1, 2)]


def swap(axis, value, odd):
    count = lax.axis_size(axis)
    pairs = odd_pairs(count) if odd else even_pairs(count)
    return lax.ppermute(value, axis, pairs + [(high, low) for low, high in pairs])


def closed(steps, spare):
    steps = list(steps)
    for source, target in spare:
        if all(source != a and target != b for a, b in steps):
            steps.append((source, target))
    return steps


def relay_steps(count, fill):
    pairs = odd_pairs(count)
    out = [(low, low + 2) for low, high in pairs] + [(high, high - 2) for low, high in pairs]
    home = [(low + 2, high) for low, high in pairs] + [(high - 2, low) for low, high in pairs]
    spares = ([(b, a) for a, b in out], out) if fill else ([], [])
    return closed(out, spares[0]), closed(home, spares[1])


def relay(axis, value, step, fill):
    count = lax.axis_size(axis)
    if count % 2 == 0:
        steps = relay_steps(count, fill)[step]
    else:
        pairs = odd_pairs(count)
        steps = [pairs + [(high, low) for low, high in pairs], [(i, i) for i in range(count)]][step]
    return lax.ppermute(value, axis, steps)


def per_device(object_tiles, probe, phase, measured, offsets, live):
    length = probe.shape[1]
    margin = length // 2
    slots = offsets.shape[0]
    high, wide = object_tiles.shape[2:]
    ext_shape = (2, high + 2 * margin, wide + 2 * margin)
    assert high == 2 * margin
    table = jnp.asarray(dft_table(length))

    def shape(*dims):
        return jax.ShapeDtypeStruct(dims, F32)

    field = shape(2, slots, length, length)
    pieces = (
        *[shape(2, 2, margin, margin)] * 2,
        *[shape(2, high, margin)] * 2,
        shape(2, high + 2 * margin, wide),
    )
    strip = shape(2, margin, wide)
    ext = pltpu.VMEM(ext_shape, F32)
    mid = pltpu.VMEM(field.shape, F32)
    stages = [
        *[pltpu.VMEM((3, length, slots * length), BF16)] * 2,
        *[pltpu.VMEM((3, slots * length, length), BF16)] * 2,
    ]
    params = pltpu.CompilerParams(vmem_limit_bytes=20 * 1024 * 1024)
    small = pltpu.CompilerParams(vmem_limit_bytes=6 * 1024 * 1024)
    cost = pl.CostEstimate(
        flops=2 * 2 * 9 * 2 * slots * length**3, bytes_accessed=8 << 20,
        transcendentals=0,
    )
    call = functools.partial(pl.pallas_call, compiler_params=params)
    call_small = functools.partial(pl.pallas_call, compiler_params=small)
    sides = shape(2, 2, high, margin)
    row_e0, row_o0, row_e1, row_o1, side_e, side_o = call_small(
        edge_kernel,
        out_shape=(*[strip] * 4, sides, sides),
        in_specs=[VMEM],
        out_specs=(VMEM,) * 6,
        name="edges",
    )(object_tiles)
    away = relay("row", row_o1, 0, True)
    halo_e0 = swap("row", row_e0, False)
    halo_o0 = swap("row", row_o0, True)
    halo_e1 = swap("row", row_e1, False)
    side_e = swap("col", side_e, False)
    side_o = swap("col", side_o, True)
    halo_o1 = relay("row", away, 1, True)
    slots_at, kernel, left, probe = call_small(
        turn_kernel,
        out_shape=(
            jax.ShapeDtypeStruct((2 * slots + 1,), jnp.int32),
            shape(2, length, length),
            jax.ShapeDtypeStruct(table.shape, BF16),
            shape(*probe.shape),
        ),
        in_specs=[SMEM] * 2 + [VMEM] * 3,
        out_specs=(SMEM, VMEM, VMEM, VMEM),
        name="turn",
    )(offsets, live, phase, table, probe)

    corners = []
    for which, halo in enumerate(((halo_e0, halo_o0), (halo_e1, halo_o1))):
        to_even, to_odd = call_small(
            cut_kernel,
            out_shape=(shape(2, 2, margin, margin),) * 2,
            in_specs=[VMEM, VMEM],
            out_specs=(VMEM, VMEM),
            name=f"cut_{which}",
        )(*halo)
        corners.append((swap("col", to_even, False), swap("col", to_odd, True)))
    near = call(
        near_kernel,
        out_shape=field,
        in_specs=[SMEM] + [VMEM] * 10,
        out_specs=VMEM,
        scratch_shapes=[ext, mid, *stages],
        cost_estimate=cost,
        name="near",
    )(
        slots_at, object_tiles, halo_e0, halo_o0, side_e, side_o, *corners[0], probe, kernel,
        left,
    )
    g_near, corner_e, corner_o, one_e, one_o, middle_one = call(
        exit_kernel,
        out_shape=(field, *pieces),
        in_specs=[SMEM] + [VMEM] * 10,
        out_specs=(VMEM,) * 6,
        scratch_shapes=[ext, ext, mid, mid, *stages],
        cost_estimate=cost,
        name="exit",
    )(
        slots_at, object_tiles, halo_e1, halo_o1, side_e, side_o, *corners[1], near,
        measured, left,
    )

    def outer_rows(name, odd, middle, corner_e, corner_o):
        return call_small(
            corner_kernel,
            out_shape=(strip, *odd),
            in_specs=[VMEM] * 3,
            out_specs=(VMEM,) * (1 + len(odd)),
            name=name,
        )(middle, corner_e, corner_o)

    corner_e = swap("col", corner_e, False)
    corner_o = swap("col", corner_o, True)
    zero_e, zero_o, side_e, side_o, middle_zero = call(
        first_kernel,
        out_shape=(*pieces[:2], sides, sides, pieces[4]),
        in_specs=[SMEM] + [VMEM] * 6,
        out_specs=(VMEM,) * 5,
        scratch_shapes=[ext, mid, *stages],
        cost_estimate=cost,
        name="first",
    )(slots_at, g_near, probe, kernel, left, one_e, one_o)
    rows_e1, rows_o1 = outer_rows("fold_one", (strip,), middle_one, corner_e, corner_o)
    rows_e1 = swap("row", rows_e1, False)
    rows_o1 = [swap("row", rows_o1, True)]
    zero_e = swap("col", zero_e, False)
    zero_o = swap("col", zero_o, True)
    rows_e0, direct, away = outer_rows(
        "fold_zero", (shape(1, margin, wide),) * 2, middle_zero, zero_e, zero_o
    )
    away = relay("row", away, 0, False)
    rows_e0 = swap("row", rows_e0, False)
    direct = swap("row", direct, True)
    rows_o0 = [direct, relay("row", away, 1, False)]
    side_e = swap("col", side_e, False)
    side_o = swap("col", side_o, True)
    whole = shape(*object_tiles.shape)
    outs = ()
    for given, steps in (
        ((middle_one, rows_e1, *rows_o1), ((1, 0, 0, [1]), (1, 1, 0, [2]))),
        ((middle_zero, rows_e0), ((0, 0, 0, [1]),)),
        ((middle_zero, *rows_o0), ((0, 1, 0, [1, 2]),)),
    ):
        rows = pltpu.VMEM((len(steps), 2, margin, wide), F32)
        outs = pl.pallas_call(
            functools.partial(final_kernel, steps),
            out_shape=(whole, whole),
            in_specs=[VMEM] * (3 + len(given)) + [ANY] * len(outs),
            out_specs=(ANY, ANY),
            scratch_shapes=[rows, rows, pltpu.SemaphoreType.DMA((len(steps), 2, 2))],
            input_output_aliases={3 + len(given): 0, 4 + len(given): 1} if outs else {},
            compiler_params=small,
        )(object_tiles, side_e, side_o, *given, *outs)
    return tuple(outs)


def solution(mesh):
    return jax.shard_map(
        per_device,
        mesh=mesh,
        in_specs=(
            P(None, None, "row", "col"),
            P(),
            P(),
            P(("row", "col"), None, None),
            P(("row", "col"), None),
            P("row", "col"),
        ),
        out_specs=(P(None, None, "row", "col"), P(None, None, "row", "col")),
        check_vma=False,
    )
```

profile of v0, /device:TPU:10, one launch (start us, length us, event | category | flops | bytes accessed | tf_op | source)
XLA Modules:
  0.0 80.9 jit_solution(7631207115073155340)
XLA Ops:
  2.0 1.6 %collective-permute-start.1 = (f32[2,128,256]{2,1,0:T(8,128)S(1)}, f32[2,128,256]{2,1,0:T(8,128)S(1)}, u32[]{:S(2)}, u32[]{:S(2)}) collective-permute-start(f32[2,128,256]{2,1,0:T(8,128)S(1)} %get-tuple-element.38), channel_id=1, source_target_pairs={{8,24},{16,0},{24,8},{0,16},{9,25},{17,1},{25,9},{1,17},{10,26},{1... | collective-permute-start | bytes 786440 | tf_op jit(solution)/shard_map/ppermute | solution.py:372
  4.1 3.3 %collective-permute-start.8 = (f32[2,128,256]{2,1,0:T(8,128)S(1)}, f32[2,128,256]{2,1,0:T(8,128)S(1)}, u32[]{:S(2)}, u32[]{:S(2)}) collective-permute-start(f32[2,128,256]{2,1,0:T(8,128)S(1)} %get-tuple-element.44), channel_id=1, source_target_pairs={{8,16},{16,8},{9,17},{17,9},{10,18},{18,10},{11,19},{19,11},{12,20... | collective-permute-start | bytes 786440 | tf_op jit(solution)/shard_map/ppermute | solution.py:346
  7.6 2.7 %collective-permute-done.1 = f32[2,128,256]{2,1,0:T(8,128)S(1)} collective-permute-done((f32[2,128,256]{2,1,0:T(8,128)S(1)}, f32[2,128,256]{2,1,0:T(8,128)S(1)}, u32[]{:S(2)}, u32[]{:S(2)}) %collective-permute-start.1) | collective-permute-done | bytes 262176 | tf_op jit(solution)/shard_map/ppermute | solution.py:372
  10.4 1.9 %collective-permute-start.4 = (f32[2,2,256,128]{3,2,1,0:T(8,128)S(1)}, f32[2,2,256,128]{3,2,1,0:T(8,128)S(1)}, u32[]{:S(2)}, u32[]{:S(2)}) collective-permute-start(f32[2,2,256,128]{3,2,1,0:T(8,128)S(1)} %get-tuple-element.40), channel_id=1, source_target_pairs={{1,2},{3,4},{5,6},{2,1},{4,3},{6,5},{9,10},{11,12},{13,14},{10,9},... | collective-permute-start | bytes 1572872 | tf_op jit(solution)/shard_map/ppermute | solution.py:346
  13.6 4.7 %collective-permute-done.8.halo_o.row_o = f32[2,128,256]{2,1,0:T(8,128)S(1)} collective-permute-done((f32[2,128,256]{2,1,0:T(8,128)S(1)}, f32[2,128,256]{2,1,0:T(8,128)S(1)}, u32[]{:S(2)}, u32[]{:S(2)}) %collective-permute-start.8) | collective-permute-done | bytes 262176 | tf_op jit(solution)/shard_map/ppermute | solution.py:346
  18.5 2.2 %collective-permute-done.halo_e.row_e = f32[2,128,256]{2,1,0:T(8,128)S(1)} collective-permute-done((f32[2,128,256]{2,1,0:T(8,128)S(1)}, f32[2,128,256]{2,1,0:T(8,128)S(1)}, u32[]{:S(2)}, u32[]{:S(2)}) %collective-permute-start) | collective-permute-done | bytes 262176 | tf_op jit(solution)/shard_map/ppermute | solution.py:346
  20.7 2.0 %collective-permute-start.10 = (f32[2,2,128,128]{3,2,1,0:T(8,128)S(1)}, f32[2,2,128,128]{3,2,1,0:T(8,128)S(1)}, u32[]{:S(2)}, u32[]{:S(2)}) collective-permute-start(f32[2,2,128,128]{3,2,1,0:T(8,128)S(1)} %get-tuple-element.46), channel_id=1, source_target_pairs={{1,2},{3,4},{5,6},{2,1},{4,3},{6,5},{9,10},{11,12},{13,14},{10,9},... | collective-permute-start | bytes 786440 | tf_op jit(solution)/shard_map/ppermute | solution.py:346
  22.8 1.7 %collective-permute-start.5 = (f32[2,2,128,128]{3,2,1,0:T(8,128)S(1)}, f32[2,2,128,128]{3,2,1,0:T(8,128)S(1)}, u32[]{:S(2)}, u32[]{:S(2)}) collective-permute-start(f32[2,2,128,128]{3,2,1,0:T(8,128)S(1)} %get-tuple-element.41), channel_id=1, source_target_pairs={{0,1},{2,3},{4,5},{6,7},{1,0},{3,2},{5,4},{7,6},{8,9},{10,11},{12,... | collective-permute-start | bytes 786440 | tf_op jit(solution)/shard_map/ppermute | solution.py:346
  24.5 2.0 %collective-permute-start.6 = (f32[2,2,128,128]{3,2,1,0:T(8,128)S(1)}, f32[2,2,128,128]{3,2,1,0:T(8,128)S(1)}, u32[]{:S(2)}, u32[]{:S(2)}) collective-permute-start(f32[2,2,128,128]{3,2,1,0:T(8,128)S(1)} %get-tuple-element.42), channel_id=1, source_target_pairs={{1,2},{3,4},{5,6},{2,1},{4,3},{6,5},{9,10},{11,12},{13,14},{10,9},... | collective-permute-start | bytes 786440 | tf_op jit(solution)/shard_map/ppermute | solution.py:346
  27.2 2.3 %turn.1 = (s32[5]{0:T(128)S(1)}, f32[2,256,256]{2,1,0:T(8,128)S(1)}, bf16[2,3,256,256]{3,2,1,0:T(8,128)(2,1)S(1)}, f32[2,256,256]{2,1,0:T(8,128)S(1)}) custom-call(s32[2,2]{1,0:T(2,128)S(1)} %copy-done.5, s32[1,1]{1,0:T(1,128)S(6)} %copy.17.live, f32[256,256]{1,0:T(8,128)S(1)} %copy-done.4, bf16[2,3,256,256]{3,2,1,0:T(8,128)(2,1)S(1)} %copy-done.2, ...), custom_call_target="tpu_custom_call" | custom-call | tf_op jit(solution)/shard_map/turn/pallas_call | solution.py:423
  29.6 4.3 %near.1 = f32[2,2,256,256]{3,2,1,0:T(8,128)S(1)} custom-call(s32[5]{0:T(128)S(1)} %get-tuple-element.36.slots_at, f32[2,2,256,256]{3,2,1,0:T(8,128)S(1)} %copy-done.1, f32[2,128,256]{2,1,0:T(8,128)S(1)} %collective-permute-done.7.halo_e.row_e, f32[2,128,256]{2,1,0:T(8,128)S(1)} %collective-permute-done.8.halo_o.row_o, ...), custom_call_target="tpu_custom_call" | custom-call | flops 2415919104 | bytes 8388608 | tf_op jit(solution)/shard_map/near/pallas_call | solution.py:446
  33.9 5.0 %exit.1 = (f32[2,2,256,256]{3,2,1,0:T(8,128)S(1)}, f32[2,2,128,128]{3,2,1,0:T(8,128)S(1)}, f32[2,2,128,128]{3,2,1,0:T(8,128)S(1)}, f32[2,256,128]{2,1,0:T(8,128)...) custom-call(s32[5]{0:T(128)S(1)} %get-tuple-element.36.slots_at, f32[2,2,256,256]{3,2,1,0:T(8,128)S(1)} %copy-done.1, ...), custom_call_target="tpu_custom_call" | custom-call | flops 2415919104 | bytes 8388608 | tf_op jit(solution)/shard_map/exit/pallas_call | solution.py:458
  38.9 4.3 %first.1 = (f32[2,2,128,128]{3,2,1,0:T(8,128)S(1)}, f32[2,2,128,128]{3,2,1,0:T(8,128)S(1)}, f32[2,2,256,128]{3,2,1,0:T(8,128)S(1)}, f32[2,2,256,128]{3,2,1,0:T(8,128)S(1)}, f32[2,512,256]{2,1,0:T(8,128)S(1)}) custom-call(s32[5]{0:T(128)S(1)} %get-tuple-element.36.slots_at, f32[2,2,256,256]{3,2,1,0:T(8,128)S(1)} %get-tuple-element.50.g_near, ...), custom_call_target="tpu_custom_call" | custom-call | flops 2415919104 | bytes 8388608 | tf_op jit(solution)/shard_map/first/pallas_call | solution.py:482
  43.2 1.7 %collective-permute-start.13 = (f32[2,2,128,128]{3,2,1,0:T(8,128)S(1)}, f32[2,2,128,128]{3,2,1,0:T(8,128)S(1)}, u32[]{:S(2)}, u32[]{:S(2)}) collective-permute-start(f32[2,2,128,128]{3,2,1,0:T(8,128)S(1)} %get-tuple-element.56), channel_id=1, source_target_pairs={{0,1},{2,3},{4,5},{6,7},{1,0},{3,2},{5,4},{7,6},{8,9},{10,11},{12,... | collective-permute-start | bytes 786440 | tf_op jit(solution)/shard_map/ppermute | solution.py:346
  44.8 2.0 %collective-permute-start.14 = (f32[2,2,128,128]{3,2,1,0:T(8,128)S(1)}, f32[2,2,128,128]{3,2,1,0:T(8,128)S(1)}, u32[]{:S(2)}, u32[]{:S(2)}) collective-permute-start(f32[2,2,128,128]{3,2,1,0:T(8,128)S(1)} %get-tuple-element.57), channel_id=1, source_target_pairs={{1,2},{3,4},{5,6},{2,1},{4,3},{6,5},{9,10},{11,12},{13,14},{10,9},... | collective-permute-start | bytes 786440 | tf_op jit(solution)/shard_map/ppermute | solution.py:346
  46.9 3.6 %collective-permute-start.20 = (f32[2,2,128,128]{3,2,1,0:T(8,128)S(1)}, f32[2,2,128,128]{3,2,1,0:T(8,128)S(1)}, u32[]{:S(2)}, u32[]{:S(2)}) collective-permute-start(f32[2,2,128,128]{3,2,1,0:T(8,128)S(1)} %get-tuple-element.63), channel_id=1, source_target_pairs={{1,2},{3,4},{5,6},{2,1},{4,3},{6,5},{9,10},{11,12},{13,14},{10,9},... | collective-permute-start | bytes 786440 | tf_op jit(solution)/shard_map/ppermute | solution.py:346
  50.6 2.0 %collective-permute-start.12 = (f32[2,2,256,128]{3,2,1,0:T(8,128)S(1)}, f32[2,2,256,128]{3,2,1,0:T(8,128)S(1)}, u32[]{:S(2)}, u32[]{:S(2)}) collective-permute-start(f32[2,2,256,128]{3,2,1,0:T(8,128)S(1)} %get-tuple-element.54), channel_id=1, source_target_pairs={{1,2},{3,4},{5,6},{2,1},{4,3},{6,5},{9,10},{11,12},{13,14},{10,9},... | collective-permute-start | bytes 1572872 | tf_op jit(solution)/shard_map/ppermute | solution.py:346
  52.7 4.4 %collective-permute-start.16 = (f32[1,128,256]{2,1,0:T(8,128)S(1)}, f32[1,128,256]{2,1,0:T(8,128)S(1)}, u32[]{:S(2)}, u32[]{:S(2)}) collective-permute-start(f32[1,128,256]{2,1,0:T(8,128)S(1)} %get-tuple-element.59), channel_id=1, source_target_pairs={{8,24},{16,0},{9,25},{17,1},{10,26},{18,2},{11,27},{19,3},{12,28},... | collective-permute-start | bytes 393224 | tf_op jit(solution)/shard_map/ppermute | solution.py:372
  58.0 3.3 %collective-permute-start.22 = (f32[2,128,256]{2,1,0:T(8,128)S(1)}, f32[2,128,256]{2,1,0:T(8,128)S(1)}, u32[]{:S(2)}, u32[]{:S(2)}) collective-permute-start(f32[2,128,256]{2,1,0:T(8,128)S(1)} %get-tuple-element.65), channel_id=1, source_target_pairs={{8,16},{16,8},{9,17},{17,9},{10,18},{18,10},{11,19},{19,11},{12,20... | collective-permute-start | bytes 786440 | tf_op jit(solution)/shard_map/ppermute | solution.py:346
  61.3 1.7 %collective-permute-start.18 = (f32[2,128,256]{2,1,0:T(8,128)S(1)}, f32[2,128,256]{2,1,0:T(8,128)S(1)}, u32[]{:S(2)}, u32[]{:S(2)}) collective-permute-start(f32[2,128,256]{2,1,0:T(8,128)S(1)} %get-tuple-element.60), channel_id=1, source_target_pairs={{0,8},{16,24},{8,0},{24,16},{1,9},{17,25},{9,1},{25,17},{2,10},{18... | collective-permute-start | bytes 786440 | tf_op jit(solution)/shard_map/ppermute | solution.py:346
  63.0 3.5 %collective-permute-done.21.refs_1_ = f32[2,128,256]{2,1,0:T(8,128)S(1)} collective-permute-done((f32[2,128,256]{2,1,0:T(8,128)S(1)}, f32[2,128,256]{2,1,0:T(8,128)S(1)}, u32[]{:S(2)}, u32[]{:S(2)}) %collective-permute-start.21) | collective-permute-done | bytes 262176 | tf_op jit(solution)/shard_map/ppermute | solution.py:346
  66.5 3.4 %collective-permute-start.15 = (f32[1,128,256]{2,1,0:T(8,128)S(1)}, f32[1,128,256]{2,1,0:T(8,128)S(1)}, u32[]{:S(2)}, u32[]{:S(2)}) collective-permute-start(f32[1,128,256]{2,1,0:T(8,128)S(1)} %get-tuple-element.58), channel_id=1, source_target_pairs={{8,16},{16,8},{9,17},{17,9},{10,18},{18,10},{11,19},{19,11},{12,20... | collective-permute-start | bytes 393224 | tf_op jit(solution)/shard_map/ppermute | solution.py:346
  69.9 2.3 %collective-permute-done.22.refs_2_ = f32[2,128,256]{2,1,0:T(8,128)S(1)} collective-permute-done((f32[2,128,256]{2,1,0:T(8,128)S(1)}, f32[2,128,256]{2,1,0:T(8,128)S(1)}, u32[]{:S(2)}, u32[]{:S(2)}) %collective-permute-start.22) | collective-permute-done | bytes 262176 | tf_op jit(solution)/shard_map/ppermute | solution.py:346
  76.8 3.2 %collective-permute-done.15.refs_1_ = f32[1,128,256]{2,1,0:T(8,128)S(1)} collective-permute-done((f32[1,128,256]{2,1,0:T(8,128)S(1)}, f32[1,128,256]{2,1,0:T(8,128)S(1)}, u32[]{:S(2)}, u32[]{:S(2)}) %collective-permute-start.15) | collective-permute-done | bytes 131104 | tf_op jit(solution)/shard_map/ppermute | solution.py:346
  (48 shorter events, 10.2 us)
Async XLA Ops:
  1.9 25.3 %copy-start.3 = (f32[2,256,256]{2,1,0:T(8,128)S(1)}, f32[2,256,256]{2,1,0:T(8,128)}, u32[]{:S(2)}) copy-start(f32[2,256,256]{2,1,0:T(8,128)} %light.1) | copy-start | bytes 1572868
  2.0 8.3 %collective-permute-start.1 = (f32[2,128,256]{2,1,0:T(8,128)S(1)}, f32[2,128,256]{2,1,0:T(8,128)S(1)}, u32[]{:S(2)}, u32[]{:S(2)}) collective-permute-start(f32[2,128,256]{2,1,0:T(8,128)S(1)} %get-tuple-element.38), channel_id=1, source_target_pairs={{8,24},{16,0},{24,8},{0,16},{9,25},{17,1},{25,9},{1,17},{10,26},{1... | collective-permute-start | bytes 786440 | tf_op jit(solution)/shard_map/ppermute | solution.py:372
  3.6 9.2 %collective-permute-start.7 = (f32[2,128,256]{2,1,0:T(8,128)S(1)}, f32[2,128,256]{2,1,0:T(8,128)S(1)}, u32[]{:S(2)}, u32[]{:S(2)}) collective-permute-start(f32[2,128,256]{2,1,0:T(8,128)S(1)} %get-tuple-element.43), channel_id=1, source_target_pairs={{0,8},{16,24},{8,0},{24,16},{1,9},{17,25},{9,1},{25,17},{2,10},{18... | collective-permute-start | bytes 786440 | tf_op jit(solution)/shard_map/ppermute | solution.py:346
  4.1 14.2 %collective-permute-start.8 = (f32[2,128,256]{2,1,0:T(8,128)S(1)}, f32[2,128,256]{2,1,0:T(8,128)S(1)}, u32[]{:S(2)}, u32[]{:S(2)}) collective-permute-start(f32[2,128,256]{2,1,0:T(8,128)S(1)} %get-tuple-element.44), channel_id=1, source_target_pairs={{8,16},{16,8},{9,17},{17,9},{10,18},{18,10},{11,19},{19,11},{12,20... | collective-permute-start | bytes 786440 | tf_op jit(solution)/shard_map/ppermute | solution.py:346
  7.5 13.2 %collective-permute-start = (f32[2,128,256]{2,1,0:T(8,128)S(1)}, f32[2,128,256]{2,1,0:T(8,128)S(1)}, u32[]{:S(2)}, u32[]{:S(2)}) collective-permute-start(f32[2,128,256]{2,1,0:T(8,128)S(1)} %get-tuple-element.37), channel_id=1, source_target_pairs={{0,8},{16,24},{8,0},{24,16},{1,9},{17,25},{9,1},{25,17},{2,10},{18... | collective-permute-start | bytes 786440 | tf_op jit(solution)/shard_map/ppermute | solution.py:346
  7.6 22.0 %collective-permute-start.3 = (f32[2,2,256,128]{3,2,1,0:T(8,128)S(1)}, f32[2,2,256,128]{3,2,1,0:T(8,128)S(1)}, u32[]{:S(2)}, u32[]{:S(2)}) collective-permute-start(f32[2,2,256,128]{3,2,1,0:T(8,128)S(1)} %get-tuple-element.39), channel_id=1, source_target_pairs={{0,1},{2,3},{4,5},{6,7},{1,0},{3,2},{5,4},{7,6},{8,9},{10,11},{12,... | collective-permute-start | bytes 1572872 | tf_op jit(solution)/shard_map/ppermute | solution.py:346
  10.4 19.2 %collective-permute-start.4 = (f32[2,2,256,128]{3,2,1,0:T(8,128)S(1)}, f32[2,2,256,128]{3,2,1,0:T(8,128)S(1)}, u32[]{:S(2)}, u32[]{:S(2)}) collective-permute-start(f32[2,2,256,128]{3,2,1,0:T(8,128)S(1)} %get-tuple-element.40), channel_id=1, source_target_pairs={{1,2},{3,4},{5,6},{2,1},{4,3},{6,5},{9,10},{11,12},{13,14},{10,9},... | collective-permute-start | bytes 1572872 | tf_op jit(solution)/shard_map/ppermute | solution.py:346
  12.8 9.9 %collective-permute-start.2 = (f32[2,128,256]{2,1,0:T(8,128)S(1)}, f32[2,128,256]{2,1,0:T(8,128)S(1)}, u32[]{:S(2)}, u32[]{:S(2)}) collective-permute-start(f32[2,128,256]{2,1,0:T(8,128)S(1)} %collective-permute-done.1), channel_id=1, source_target_pairs={{24,16},{0,8},{8,24},{16,0},{25,17},{1,9},{9,25},{17,1},{26,18},{2... | collective-permute-start | bytes 786440 | tf_op jit(solution)/shard_map/ppermute | solution.py:372
  18.4 6.1 %collective-permute-start.9 = (f32[2,2,128,128]{3,2,1,0:T(8,128)S(1)}, f32[2,2,128,128]{3,2,1,0:T(8,128)S(1)}, u32[]{:S(2)}, u32[]{:S(2)}) collective-permute-start(f32[2,2,128,128]{3,2,1,0:T(8,128)S(1)} %get-tuple-element.45), channel_id=1, source_target_pairs={{0,1},{2,3},{4,5},{6,7},{1,0},{3,2},{5,4},{7,6},{8,9},{10,11},{12,... | collective-permute-start | bytes 786440 | tf_op jit(solution)/shard_map/ppermute | solution.py:346
  20.7 8.9 %collective-permute-start.10 = (f32[2,2,128,128]{3,2,1,0:T(8,128)S(1)}, f32[2,2,128,128]{3,2,1,0:T(8,128)S(1)}, u32[]{:S(2)}, u32[]{:S(2)}) collective-permute-start(f32[2,2,128,128]{3,2,1,0:T(8,128)S(1)} %get-tuple-element.46), channel_id=1, source_target_pairs={{1,2},{3,4},{5,6},{2,1},{4,3},{6,5},{9,10},{11,12},{13,14},{10,9},... | collective-permute-start | bytes 786440 | tf_op jit(solution)/shard_map/ppermute | solution.py:346
  22.8 11.1 %collective-permute-start.5 = (f32[2,2,128,128]{3,2,1,0:T(8,128)S(1)}, f32[2,2,128,128]{3,2,1,0:T(8,128)S(1)}, u32[]{:S(2)}, u32[]{:S(2)}) collective-permute-start(f32[2,2,128,128]{3,2,1,0:T(8,128)S(1)} %get-tuple-element.41), channel_id=1, source_target_pairs={{0,1},{2,3},{4,5},{6,7},{1,0},{3,2},{5,4},{7,6},{8,9},{10,11},{12,... | collective-permute-start | bytes 786440 | tf_op jit(solution)/shard_map/ppermute | solution.py:346
  24.5 9.4 %collective-permute-start.6 = (f32[2,2,128,128]{3,2,1,0:T(8,128)S(1)}, f32[2,2,128,128]{3,2,1,0:T(8,128)S(1)}, u32[]{:S(2)}, u32[]{:S(2)}) collective-permute-start(f32[2,2,128,128]{3,2,1,0:T(8,128)S(1)} %get-tuple-element.42), channel_id=1, source_target_pairs={{1,2},{3,4},{5,6},{2,1},{4,3},{6,5},{9,10},{11,12},{13,14},{10,9},... | collective-permute-start | bytes 786440 | tf_op jit(solution)/shard_map/ppermute | solution.py:346
  43.2 7.4 %collective-permute-start.13 = (f32[2,2,128,128]{3,2,1,0:T(8,128)S(1)}, f32[2,2,128,128]{3,2,1,0:T(8,128)S(1)}, u32[]{:S(2)}, u32[]{:S(2)}) collective-permute-start(f32[2,2,128,128]{3,2,1,0:T(8,128)S(1)} %get-tuple-element.56), channel_id=1, source_target_pairs={{0,1},{2,3},{4,5},{6,7},{1,0},{3,2},{5,4},{7,6},{8,9},{10,11},{12,... | collective-permute-start | bytes 786440 | tf_op jit(solution)/shard_map/ppermute | solution.py:346
  44.8 7.7 %collective-permute-start.14 = (f32[2,2,128,128]{3,2,1,0:T(8,128)S(1)}, f32[2,2,128,128]{3,2,1,0:T(8,128)S(1)}, u32[]{:S(2)}, u32[]{:S(2)}) collective-permute-start(f32[2,2,128,128]{3,2,1,0:T(8,128)S(1)} %get-tuple-element.57), channel_id=1, source_target_pairs={{1,2},{3,4},{5,6},{2,1},{4,3},{6,5},{9,10},{11,12},{13,14},{10,9},... | collective-permute-start | bytes 786440 | tf_op jit(solution)/shard_map/ppermute | solution.py:346
  46.8 10.3 %collective-permute-start.19 = (f32[2,2,128,128]{3,2,1,0:T(8,128)S(1)}, f32[2,2,128,128]{3,2,1,0:T(8,128)S(1)}, u32[]{:S(2)}, u32[]{:S(2)}) collective-permute-start(f32[2,2,128,128]{3,2,1,0:T(8,128)S(1)} %get-tuple-element.62), channel_id=1, source_target_pairs={{0,1},{2,3},{4,5},{6,7},{1,0},{3,2},{5,4},{7,6},{8,9},{10,11},{12,... | collective-permute-start | bytes 786440 | tf_op jit(solution)/shard_map/ppermute | solution.py:346
  46.9 10.2 %collective-permute-start.20 = (f32[2,2,128,128]{3,2,1,0:T(8,128)S(1)}, f32[2,2,128,128]{3,2,1,0:T(8,128)S(1)}, u32[]{:S(2)}, u32[]{:S(2)}) collective-permute-start(f32[2,2,128,128]{3,2,1,0:T(8,128)S(1)} %get-tuple-element.63), channel_id=1, source_target_pairs={{1,2},{3,4},{5,6},{2,1},{4,3},{6,5},{9,10},{11,12},{13,14},{10,9},... | collective-permute-start | bytes 786440 | tf_op jit(solution)/shard_map/ppermute | solution.py:346
  50.5 23.0 %collective-permute-start.11 = (f32[2,2,256,128]{3,2,1,0:T(8,128)S(1)}, f32[2,2,256,128]{3,2,1,0:T(8,128)S(1)}, u32[]{:S(2)}, u32[]{:S(2)}) collective-permute-start(f32[2,2,256,128]{3,2,1,0:T(8,128)S(1)} %get-tuple-element.53), channel_id=1, source_target_pairs={{0,1},{2,3},{4,5},{6,7},{1,0},{3,2},{5,4},{7,6},{8,9},{10,11},{12,... | collective-permute-start | bytes 1572872 | tf_op jit(solution)/shard_map/ppermute | solution.py:346
  50.6 22.9 %collective-permute-start.12 = (f32[2,2,256,128]{3,2,1,0:T(8,128)S(1)}, f32[2,2,256,128]{3,2,1,0:T(8,128)S(1)}, u32[]{:S(2)}, u32[]{:S(2)}) collective-permute-start(f32[2,2,256,128]{3,2,1,0:T(8,128)S(1)} %get-tuple-element.54), channel_id=1, source_target_pairs={{1,2},{3,4},{5,6},{2,1},{4,3},{6,5},{9,10},{11,12},{13,14},{10,9},... | collective-permute-start | bytes 1572872 | tf_op jit(solution)/shard_map/ppermute | solution.py:346
  52.7 8.6 %collective-permute-start.16 = (f32[1,128,256]{2,1,0:T(8,128)S(1)}, f32[1,128,256]{2,1,0:T(8,128)S(1)}, u32[]{:S(2)}, u32[]{:S(2)}) collective-permute-start(f32[1,128,256]{2,1,0:T(8,128)S(1)} %get-tuple-element.59), channel_id=1, source_target_pairs={{8,24},{16,0},{9,25},{17,1},{10,26},{18,2},{11,27},{19,3},{12,28},... | collective-permute-start | bytes 393224 | tf_op jit(solution)/shard_map/ppermute | solution.py:372
  57.3 9.2 %collective-permute-start.21 = (f32[2,128,256]{2,1,0:T(8,128)S(1)}, f32[2,128,256]{2,1,0:T(8,128)S(1)}, u32[]{:S(2)}, u32[]{:S(2)}) collective-permute-start(f32[2,128,256]{2,1,0:T(8,128)S(1)} %get-tuple-element.64), channel_id=1, source_target_pairs={{0,8},{16,24},{8,0},{24,16},{1,9},{17,25},{9,1},{25,17},{2,10},{18... | collective-permute-start | bytes 786440 | tf_op jit(solution)/shard_map/ppermute | solution.py:346
  58.0 14.2 %collective-permute-start.22 = (f32[2,128,256]{2,1,0:T(8,128)S(1)}, f32[2,128,256]{2,1,0:T(8,128)S(1)}, u32[]{:S(2)}, u32[]{:S(2)}) collective-permute-start(f32[2,128,256]{2,1,0:T(8,128)S(1)} %get-tuple-element.65), channel_id=1, source_target_pairs={{8,16},{16,8},{9,17},{17,9},{10,18},{18,10},{11,19},{19,11},{12,20... | collective-permute-start | bytes 786440 | tf_op jit(solution)/shard_map/ppermute | solution.py:346
  61.3 14.6 %collective-permute-start.18 = (f32[2,128,256]{2,1,0:T(8,128)S(1)}, f32[2,128,256]{2,1,0:T(8,128)S(1)}, u32[]{:S(2)}, u32[]{:S(2)}) collective-permute-start(f32[2,128,256]{2,1,0:T(8,128)S(1)} %get-tuple-element.60), channel_id=1, source_target_pairs={{0,8},{16,24},{8,0},{24,16},{1,9},{17,25},{9,1},{25,17},{2,10},{18... | collective-permute-start | bytes 786440 | tf_op jit(solution)/shard_map/ppermute | solution.py:346
  66.5 13.5 %collective-permute-start.15 = (f32[1,128,256]{2,1,0:T(8,128)S(1)}, f32[1,128,256]{2,1,0:T(8,128)S(1)}, u32[]{:S(2)}, u32[]{:S(2)}) collective-permute-start(f32[1,128,256]{2,1,0:T(8,128)S(1)} %get-tuple-element.58), channel_id=1, source_target_pairs={{8,16},{16,8},{9,17},{17,9},{10,18},{18,10},{11,19},{19,11},{12,20... | collective-permute-start | bytes 393224 | tf_op jit(solution)/shard_map/ppermute | solution.py:346
  72.2 7.8 %collective-permute-start.17 = (f32[1,128,256]{2,1,0:T(8,128)S(1)}, f32[1,128,256]{2,1,0:T(8,128)S(1)}, u32[]{:S(2)}, u32[]{:S(2)}) collective-permute-start(f32[1,128,256]{2,1,0:T(8,128)S(1)} %collective-permute-done.16), channel_id=1, source_target_pairs={{24,16},{0,8},{25,17},{1,9},{26,18},{2,10},{27,19},{3,11},{28,20},... | collective-permute-start | bytes 393224 | tf_op jit(solution)/shard_map/ppermute | solution.py:372
  (6 other events, 55.0 us)
where the time goes:
time: 81.3 us; the launch traced here: 80.9 us
  starting transfers between devices  38.3 us (47%)
  waiting for transfers between devices  20.4 us (25%)
  Pallas kernels  19.2 us (24%)
  between operations  1.63 us (2%)
  local copies, waits for them, and re-layouts  1.25 us (2%)
    ppermute x19, starting transfers between devices, swap(): lax.ppermute(value, axis, pairs + [(high, low) for low, high in pairs])  30.2 us
    ppermute x19, waiting for transfers between devices, swap(): lax.ppermute(value, axis, pairs + [(high, low) for low, high in pairs])  17.7 us
    ppermute x4, starting transfers between devices, relay(): return lax.ppermute(value, axis, steps)  8.09 us
    pallas_call x1, Pallas kernels, per_device(): call(exit_kernel, out_shape=(field, *pieces), in_specs=[SMEM] + [VMEM] *...  4.99 us
    pallas_call x1, Pallas kernels, per_device(): call(near_kernel, out_shape=field, in_specs=[SMEM] + [VMEM] * 10, out_spe...  4.29 us
    pallas_call x1, Pallas kernels, per_device(): call(first_kernel, out_shape=(*pieces[:2], sides, sides, pieces[4]), in_s...  4.26 us
    pallas_call x3, Pallas kernels, per_device(): pl.pallas_call(functools.partial(final_kernel, steps), out_shape=(whole,...  2.87 us
    ppermute x4, waiting for transfers between devices, relay(): return lax.ppermute(value, axis, steps)  2.73 us
  transfers between devices with their start and end apart: 23, of which 8 were waited for; matrix products, arithmetic and copies ran while one was open for 0% of the time, Pallas kernels for 11%

commit v1 on v0

--- a/solution.py
+++ b/solution.py
@@ -119,10 +119,14 @@
         middle[part] = gext[part, :, inner_cols]
 
 
+def scalar(slots_at, index):
+    return jnp.max(slots_at[pl.ds(index, 1), :]).astype(jnp.int32)
+
+
 def place(slots_at, slot, shape, length):
     spans, shifts = ([], [])
     for axis, tile in ((0, 8), (1, 128)):
-        at = slots_at[2 * slot + axis]
+        at = scalar(slots_at, 2 * slot + axis)
         base = jnp.minimum(at // tile, (shape[axis + 1] - length) // tile - 1)
         spans.append(pl.ds(pl.multiple_of(base * tile, tile), length + tile))
         shifts.append(at - base * tile)
@@ -220,7 +224,7 @@
         return multiply((near[0, slot], near[1, slot]), (cut[0, slot], cut[1, slot]))
 
     def residual(slot, re, im):
-        weight = jnp.where(slot < slots_at[2 * near.shape[1]], 1.0, 0.0).astype(F32)
+        weight = jnp.where(slot < scalar(slots_at, 2 * near.shape[1]), 1.0, 0.0).astype(F32)
         factor = weight * (re * re + im * im - measured[slot])
         put(mid, slot, factor * re, factor * im)
 
@@ -322,10 +326,13 @@
 
 
 def turn_kernel(offsets, live, phase, table, light, slots_at, kernel, left, probe):
-    for slot in range(offsets.shape[0]):
-        for axis in range(2):
-            slots_at[2 * slot + axis] = offsets[slot, axis]
-    slots_at[2 * offsets.shape[0]] = live[0, 0]
+    count = offsets.shape[0]
+    scalars = [offsets[slot, axis] for slot in range(count) for axis in range(2)] + [live[0, 0]]
+    row = lax.broadcasted_iota(jnp.int32, slots_at.shape, 0)
+    total = jnp.zeros(slots_at.shape, jnp.int32)
+    for index, scalar in enumerate(scalars):
+        total = jnp.where(row == index, scalar, total)
+    slots_at[...] = total.astype(F32)
     left[...] = table[...]
     probe[...] = light[...]
     kernel[0] = jnp.cos(phase[...])
@@ -423,13 +430,13 @@
     slots_at, kernel, left, probe = call_small(
         turn_kernel,
         out_shape=(
-            jax.ShapeDtypeStruct((2 * slots + 1,), jnp.int32),
+            shape(8 * pl.cdiv(2 * slots + 1, 8), 128),
             shape(2, length, length),
             jax.ShapeDtypeStruct(table.shape, BF16),
             shape(*probe.shape),
         ),
         in_specs=[SMEM] * 2 + [VMEM] * 3,
-        out_specs=(SMEM, VMEM, VMEM, VMEM),
+        out_specs=(VMEM,) * 4,
         name="turn",
     )(offsets, live, phase, table, probe)
 
@@ -446,7 +453,7 @@
     near = call(
         near_kernel,
         out_shape=field,
-        in_specs=[SMEM] + [VMEM] * 10,
+        in_specs=[VMEM] * 11,
         out_specs=VMEM,
         scratch_shapes=[ext, mid, *stages],
         cost_estimate=cost,
@@ -458,7 +465,7 @@
     g_near, corner_e, corner_o, one_e, one_o, middle_one = call(
         exit_kernel,
         out_shape=(field, *pieces),
-        in_specs=[SMEM] + [VMEM] * 10,
+        in_specs=[VMEM] * 11,
         out_specs=(VMEM,) * 6,
         scratch_shapes=[ext, ext, mid, mid, *stages],
         cost_estimate=cost,
@@ -482,7 +489,7 @@
     zero_e, zero_o, side_e, side_o, middle_zero = call(
         first_kernel,
         out_shape=(*pieces[:2], sides, sides, pieces[4]),
-        in_specs=[SMEM] + [VMEM] * 6,
+        in_specs=[VMEM] * 7,
         out_specs=(VMEM,) * 5,
         scratch_shapes=[ext, mid, *stages],
         cost_estimate=cost,

time: 81.3 us -> 79.6 us (0.979)
  Pallas kernels: 19.2 us -> 17.5 us
    pallas_call x3, Pallas kernels: 11.6 us -> 10.5 us  [the longest x1 4.44 us: per_device(): call(exit_kernel, out_shape=(field, *pieces), in_specs=[VMEM] * 11, out_s...]
where the time goes in v1:
time: 79.6 us; the launch traced here: 79.2 us
  starting transfers between devices  38.3 us (48%)
  waiting for transfers between devices  20.5 us (26%)
  Pallas kernels  17.5 us (22%)
  between operations  1.63 us (2%)
  local copies, waits for them, and re-layouts  1.25 us (2%)
    ppermute x19, starting transfers between devices, swap(): lax.ppermute(value, axis, pairs + [(high, low) for low, high in pairs])  30.2 us
    ppermute x19, waiting for transfers between devices, swap(): lax.ppermute(value, axis, pairs + [(high, low) for low, high in pairs])  17.7 us
    ppermute x4, starting transfers between devices, relay(): return lax.ppermute(value, axis, steps)  8.07 us
    pallas_call x1, Pallas kernels, per_device(): call(exit_kernel, out_shape=(field, *pieces), in_specs=[VMEM] * 11, out_s...  4.44 us
    pallas_call x1, Pallas kernels, per_device(): call(first_kernel, out_shape=(*pieces[:2], sides, sides, pieces[4]), in_s...  3.72 us
    pallas_call x1, Pallas kernels, per_device(): call(near_kernel, out_shape=field, in_specs=[VMEM] * 11, out_specs=VMEM,...  3.72 us
    pallas_call x3, Pallas kernels, per_device(): pl.pallas_call(functools.partial(final_kernel, steps), out_shape=(whole,...  2.87 us
    ppermute x4, waiting for transfers between devices, relay(): return lax.ppermute(value, axis, steps)  2.73 us
  transfers between devices with their start and end apart: 23, of which 8 were waited for; matrix products, arithmetic and copies ran while one was open for 0% of the time, Pallas kernels for 11%

profile of v1, /device:TPU:10, one launch (start us, length us, event | category | flops | bytes accessed | tf_op | source)
XLA Modules:
  0.0 79.2 jit_solution(16702453860839274768)
XLA Ops:
  2.0 1.6 %collective-permute-start.1 = (f32[2,128,256]{2,1,0:T(8,128)S(1)}, f32[2,128,256]{2,1,0:T(8,128)S(1)}, u32[]{:S(2)}, u32[]{:S(2)}) collective-permute-start(f32[2,128,256]{2,1,0:T(8,128)S(1)} %get-tuple-element.38), channel_id=1, source_target_pairs={{8,24},{16,0},{24,8},{0,16},{9,25},{17,1},{25,9},{1,17},{10,26},{1... | collective-permute-start | bytes 786440 | tf_op jit(solution)/shard_map/ppermute | solution.py:379
  4.1 3.3 %collective-permute-start.8 = (f32[2,128,256]{2,1,0:T(8,128)S(1)}, f32[2,128,256]{2,1,0:T(8,128)S(1)}, u32[]{:S(2)}, u32[]{:S(2)}) collective-permute-start(f32[2,128,256]{2,1,0:T(8,128)S(1)} %get-tuple-element.44), channel_id=1, source_target_pairs={{8,16},{16,8},{9,17},{17,9},{10,18},{18,10},{11,19},{19,11},{12,20... | collective-permute-start | bytes 786440 | tf_op jit(solution)/shard_map/ppermute | solution.py:353
  7.6 2.7 %collective-permute-done.1 = f32[2,128,256]{2,1,0:T(8,128)S(1)} collective-permute-done((f32[2,128,256]{2,1,0:T(8,128)S(1)}, f32[2,128,256]{2,1,0:T(8,128)S(1)}, u32[]{:S(2)}, u32[]{:S(2)}) %collective-permute-start.1) | collective-permute-done | bytes 262176 | tf_op jit(solution)/shard_map/ppermute | solution.py:379
  10.4 1.9 %collective-permute-start.4 = (f32[2,2,256,128]{3,2,1,0:T(8,128)S(1)}, f32[2,2,256,128]{3,2,1,0:T(8,128)S(1)}, u32[]{:S(2)}, u32[]{:S(2)}) collective-permute-start(f32[2,2,256,128]{3,2,1,0:T(8,128)S(1)} %get-tuple-element.40), channel_id=1, source_target_pairs={{1,2},{3,4},{5,6},{2,1},{4,3},{6,5},{9,10},{11,12},{13,14},{10,9},... | collective-permute-start | bytes 1572872 | tf_op jit(solution)/shard_map/ppermute | solution.py:353
  13.6 4.7 %collective-permute-done.8.halo_o.row_o = f32[2,128,256]{2,1,0:T(8,128)S(1)} collective-permute-done((f32[2,128,256]{2,1,0:T(8,128)S(1)}, f32[2,128,256]{2,1,0:T(8,128)S(1)}, u32[]{:S(2)}, u32[]{:S(2)}) %collective-permute-start.8) | collective-permute-done | bytes 262176 | tf_op jit(solution)/shard_map/ppermute | solution.py:353
  18.5 2.2 %collective-permute-done.halo_e.row_e = f32[2,128,256]{2,1,0:T(8,128)S(1)} collective-permute-done((f32[2,128,256]{2,1,0:T(8,128)S(1)}, f32[2,128,256]{2,1,0:T(8,128)S(1)}, u32[]{:S(2)}, u32[]{:S(2)}) %collective-permute-start) | collective-permute-done | bytes 262176 | tf_op jit(solution)/shard_map/ppermute | solution.py:353
  20.7 2.0 %collective-permute-start.10 = (f32[2,2,128,128]{3,2,1,0:T(8,128)S(1)}, f32[2,2,128,128]{3,2,1,0:T(8,128)S(1)}, u32[]{:S(2)}, u32[]{:S(2)}) collective-permute-start(f32[2,2,128,128]{3,2,1,0:T(8,128)S(1)} %get-tuple-element.46), channel_id=1, source_target_pairs={{1,2},{3,4},{5,6},{2,1},{4,3},{6,5},{9,10},{11,12},{13,14},{10,9},... | collective-permute-start | bytes 786440 | tf_op jit(solution)/shard_map/ppermute | solution.py:353
  22.8 1.7 %collective-permute-start.5 = (f32[2,2,128,128]{3,2,1,0:T(8,128)S(1)}, f32[2,2,128,128]{3,2,1,0:T(8,128)S(1)}, u32[]{:S(2)}, u32[]{:S(2)}) collective-permute-start(f32[2,2,128,128]{3,2,1,0:T(8,128)S(1)} %get-tuple-element.41), channel_id=1, source_target_pairs={{0,1},{2,3},{4,5},{6,7},{1,0},{3,2},{5,4},{7,6},{8,9},{10,11},{12,... | collective-permute-start | bytes 786440 | tf_op jit(solution)/shard_map/ppermute | solution.py:353
  24.5 2.0 %collective-permute-start.6 = (f32[2,2,128,128]{3,2,1,0:T(8,128)S(1)}, f32[2,2,128,128]{3,2,1,0:T(8,128)S(1)}, u32[]{:S(2)}, u32[]{:S(2)}) collective-permute-start(f32[2,2,128,128]{3,2,1,0:T(8,128)S(1)} %get-tuple-element.42), channel_id=1, source_target_pairs={{1,2},{3,4},{5,6},{2,1},{4,3},{6,5},{9,10},{11,12},{13,14},{10,9},... | collective-permute-start | bytes 786440 | tf_op jit(solution)/shard_map/ppermute | solution.py:353
  27.2 2.3 %turn.1 = (f32[8,128]{1,0:T(8,128)S(1)}, f32[2,256,256]{2,1,0:T(8,128)S(1)}, bf16[2,3,256,256]{3,2,1,0:T(8,128)(2,1)S(1)}, f32[2,256,256]{2,1,0:T(8,128)S(1)}) custom-call(s32[2,2]{1,0:T(2,128)S(1)} %copy-done.5, s32[1,1]{1,0:T(1,128)S(6)} %copy.17.live, f32[256,256]{1,0:T(8,128)S(1)} %copy-done.4, bf16[2,3,256,256]{3,2,1,0:T(8,128)(2,1)S(1)} %copy-done.2, ...), custom_call_target="tpu_custom_call" | custom-call | tf_op jit(solution)/shard_map/turn/pallas_call | solution.py:430
  29.6 3.7 %near.1 = f32[2,2,256,256]{3,2,1,0:T(8,128)S(1)} custom-call(f32[8,128]{1,0:T(8,128)S(1)} %get-tuple-element.36.slots_at, f32[2,2,256,256]{3,2,1,0:T(8,128)S(1)} %copy-done.1, f32[2,128,256]{2,1,0:T(8,128)S(1)} %collective-permute-done.7.halo_e.row_e, f32[2,128,256]{2,1,0:T(8,128)S(1)} %collective-permute-done.8.halo_o.row_o, ...), custom_call_target="tpu_custom_call" | custom-call | flops 2415919104 | bytes 8388608 | tf_op jit(solution)/shard_map/near/pallas_call | solution.py:453
  33.3 4.4 %exit.1 = (f32[2,2,256,256]{3,2,1,0:T(8,128)S(1)}, f32[2,2,128,128]{3,2,1,0:T(8,128)S(1)}, f32[2,2,128,128]{3,2,1,0:T(8,128)S(1)}, f32[2,256,128]{2,1,0:T(8,128)...) custom-call(f32[8,128]{1,0:T(8,128)S(1)} %get-tuple-element.36.slots_at, f32[2,2,256,256]{3,2,1,0:T(8,128)S(1)} %copy-done.1, ...), custom_call_target="tpu_custom_call" | custom-call | flops 2415919104 | bytes 8388608 | tf_op jit(solution)/shard_map/exit/pallas_call | solution.py:465
  37.8 3.7 %first.1 = (f32[2,2,128,128]{3,2,1,0:T(8,128)S(1)}, f32[2,2,128,128]{3,2,1,0:T(8,128)S(1)}, f32[2,2,256,128]{3,2,1,0:T(8,128)S(1)}, f32[2,2,256,128]{3,2,1,0:T(8,128)S(1)}, f32[2,512,256]{2,1,0:T(8,128)S(1)}) custom-call(f32[8,128]{1,0:T(8,128)S(1)} %get-tuple-element.36.slots_at, f32[2,2,256,256]{3,2,1,0:T(8,128)S(1)} %get-tuple-element.50.g_near, ...), custom_call_target="tpu_custom_call" | custom-call | flops 2415919104 | bytes 8388608 | tf_op jit(solution)/shard_map/first/pallas_call | solution.py:489
  41.5 1.7 %collective-permute-start.13 = (f32[2,2,128,128]{3,2,1,0:T(8,128)S(1)}, f32[2,2,128,128]{3,2,1,0:T(8,128)S(1)}, u32[]{:S(2)}, u32[]{:S(2)}) collective-permute-start(f32[2,2,128,128]{3,2,1,0:T(8,128)S(1)} %get-tuple-element.56), channel_id=1, source_target_pairs={{0,1},{2,3},{4,5},{6,7},{1,0},{3,2},{5,4},{7,6},{8,9},{10,11},{12,... | collective-permute-start | bytes 786440 | tf_op jit(solution)/shard_map/ppermute | solution.py:353
  43.2 2.0 %collective-permute-start.14 = (f32[2,2,128,128]{3,2,1,0:T(8,128)S(1)}, f32[2,2,128,128]{3,2,1,0:T(8,128)S(1)}, u32[]{:S(2)}, u32[]{:S(2)}) collective-permute-start(f32[2,2,128,128]{3,2,1,0:T(8,128)S(1)} %get-tuple-element.57), channel_id=1, source_target_pairs={{1,2},{3,4},{5,6},{2,1},{4,3},{6,5},{9,10},{11,12},{13,14},{10,9},... | collective-permute-start | bytes 786440 | tf_op jit(solution)/shard_map/ppermute | solution.py:353
  45.3 3.5 %collective-permute-start.20 = (f32[2,2,128,128]{3,2,1,0:T(8,128)S(1)}, f32[2,2,128,128]{3,2,1,0:T(8,128)S(1)}, u32[]{:S(2)}, u32[]{:S(2)}) collective-permute-start(f32[2,2,128,128]{3,2,1,0:T(8,128)S(1)} %get-tuple-element.63), channel_id=1, source_target_pairs={{1,2},{3,4},{5,6},{2,1},{4,3},{6,5},{9,10},{11,12},{13,14},{10,9},... | collective-permute-start | bytes 786440 | tf_op jit(solution)/shard_map/ppermute | solution.py:353
  48.9 2.0 %collective-permute-start.12 = (f32[2,2,256,128]{3,2,1,0:T(8,128)S(1)}, f32[2,2,256,128]{3,2,1,0:T(8,128)S(1)}, u32[]{:S(2)}, u32[]{:S(2)}) collective-permute-start(f32[2,2,256,128]{3,2,1,0:T(8,128)S(1)} %get-tuple-element.54), channel_id=1, source_target_pairs={{1,2},{3,4},{5,6},{2,1},{4,3},{6,5},{9,10},{11,12},{13,14},{10,9},... | collective-permute-start | bytes 1572872 | tf_op jit(solution)/shard_map/ppermute | solution.py:353
  51.1 4.4 %collective-permute-start.16 = (f32[1,128,256]{2,1,0:T(8,128)S(1)}, f32[1,128,256]{2,1,0:T(8,128)S(1)}, u32[]{:S(2)}, u32[]{:S(2)}) collective-permute-start(f32[1,128,256]{2,1,0:T(8,128)S(1)} %get-tuple-element.59), channel_id=1, source_target_pairs={{8,24},{16,0},{9,25},{17,1},{10,26},{18,2},{11,27},{19,3},{12,28},... | collective-permute-start | bytes 393224 | tf_op jit(solution)/shard_map/ppermute | solution.py:379
  56.3 3.3 %collective-permute-start.22 = (f32[2,128,256]{2,1,0:T(8,128)S(1)}, f32[2,128,256]{2,1,0:T(8,128)S(1)}, u32[]{:S(2)}, u32[]{:S(2)}) collective-permute-start(f32[2,128,256]{2,1,0:T(8,128)S(1)} %get-tuple-element.65), channel_id=1, source_target_pairs={{8,16},{16,8},{9,17},{17,9},{10,18},{18,10},{11,19},{19,11},{12,20... | collective-permute-start | bytes 786440 | tf_op jit(solution)/shard_map/ppermute | solution.py:353
  59.7 1.6 %collective-permute-start.18 = (f32[2,128,256]{2,1,0:T(8,128)S(1)}, f32[2,128,256]{2,1,0:T(8,128)S(1)}, u32[]{:S(2)}, u32[]{:S(2)}) collective-permute-start(f32[2,128,256]{2,1,0:T(8,128)S(1)} %get-tuple-element.60), channel_id=1, source_target_pairs={{0,8},{16,24},{8,0},{24,16},{1,9},{17,25},{9,1},{25,17},{2,10},{18... | collective-permute-start | bytes 786440 | tf_op jit(solution)/shard_map/ppermute | solution.py:353
  61.3 3.5 %collective-permute-done.21.refs_1_ = f32[2,128,256]{2,1,0:T(8,128)S(1)} collective-permute-done((f32[2,128,256]{2,1,0:T(8,128)S(1)}, f32[2,128,256]{2,1,0:T(8,128)S(1)}, u32[]{:S(2)}, u32[]{:S(2)}) %collective-permute-start.21) | collective-permute-done | bytes 262176 | tf_op jit(solution)/shard_map/ppermute | solution.py:353
  64.8 3.4 %collective-permute-start.15 = (f32[1,128,256]{2,1,0:T(8,128)S(1)}, f32[1,128,256]{2,1,0:T(8,128)S(1)}, u32[]{:S(2)}, u32[]{:S(2)}) collective-permute-start(f32[1,128,256]{2,1,0:T(8,128)S(1)} %get-tuple-element.58), channel_id=1, source_target_pairs={{8,16},{16,8},{9,17},{17,9},{10,18},{18,10},{11,19},{19,11},{12,20... | collective-permute-start | bytes 393224 | tf_op jit(solution)/shard_map/ppermute | solution.py:353
  68.2 2.3 %collective-permute-done.22.refs_2_ = f32[2,128,256]{2,1,0:T(8,128)S(1)} collective-permute-done((f32[2,128,256]{2,1,0:T(8,128)S(1)}, f32[2,128,256]{2,1,0:T(8,128)S(1)}, u32[]{:S(2)}, u32[]{:S(2)}) %collective-permute-start.22) | collective-permute-done | bytes 262176 | tf_op jit(solution)/shard_map/ppermute | solution.py:353
  75.1 3.2 %collective-permute-done.15.refs_1_ = f32[1,128,256]{2,1,0:T(8,128)S(1)} collective-permute-done((f32[1,128,256]{2,1,0:T(8,128)S(1)}, f32[1,128,256]{2,1,0:T(8,128)S(1)}, u32[]{:S(2)}, u32[]{:S(2)}) %collective-permute-start.15) | collective-permute-done | bytes 131104 | tf_op jit(solution)/shard_map/ppermute | solution.py:353
  (48 shorter events, 10.2 us)
Async XLA Ops:
  1.9 25.3 %copy-start.3 = (f32[2,256,256]{2,1,0:T(8,128)S(1)}, f32[2,256,256]{2,1,0:T(8,128)}, u32[]{:S(2)}) copy-start(f32[2,256,256]{2,1,0:T(8,128)} %light.1) | copy-start | bytes 1572868
  2.0 8.3 %collective-permute-start.1 = (f32[2,128,256]{2,1,0:T(8,128)S(1)}, f32[2,128,256]{2,1,0:T(8,128)S(1)}, u32[]{:S(2)}, u32[]{:S(2)}) collective-permute-start(f32[2,128,256]{2,1,0:T(8,128)S(1)} %get-tuple-element.38), channel_id=1, source_target_pairs={{8,24},{16,0},{24,8},{0,16},{9,25},{17,1},{25,9},{1,17},{10,26},{1... | collective-permute-start | bytes 786440 | tf_op jit(solution)/shard_map/ppermute | solution.py:379
  3.6 9.2 %collective-permute-start.7 = (f32[2,128,256]{2,1,0:T(8,128)S(1)}, f32[2,128,256]{2,1,0:T(8,128)S(1)}, u32[]{:S(2)}, u32[]{:S(2)}) collective-permute-start(f32[2,128,256]{2,1,0:T(8,128)S(1)} %get-tuple-element.43), channel_id=1, source_target_pairs={{0,8},{16,24},{8,0},{24,16},{1,9},{17,25},{9,1},{25,17},{2,10},{18... | collective-permute-start | bytes 786440 | tf_op jit(solution)/shard_map/ppermute | solution.py:353
  4.1 14.2 %collective-permute-start.8 = (f32[2,128,256]{2,1,0:T(8,128)S(1)}, f32[2,128,256]{2,1,0:T(8,128)S(1)}, u32[]{:S(2)}, u32[]{:S(2)}) collective-permute-start(f32[2,128,256]{2,1,0:T(8,128)S(1)} %get-tuple-element.44), channel_id=1, source_target_pairs={{8,16},{16,8},{9,17},{17,9},{10,18},{18,10},{11,19},{19,11},{12,20... | collective-permute-start | bytes 786440 | tf_op jit(solution)/shard_map/ppermute | solution.py:353
  7.5 13.2 %collective-permute-start = (f32[2,128,256]{2,1,0:T(8,128)S(1)}, f32[2,128,256]{2,1,0:T(8,128)S(1)}, u32[]{:S(2)}, u32[]{:S(2)}) collective-permute-start(f32[2,128,256]{2,1,0:T(8,128)S(1)} %get-tuple-element.37), channel_id=1, source_target_pairs={{0,8},{16,24},{8,0},{24,16},{1,9},{17,25},{9,1},{25,17},{2,10},{18... | collective-permute-start | bytes 786440 | tf_op jit(solution)/shard_map/ppermute | solution.py:353
  7.6 22.0 %collective-permute-start.3 = (f32[2,2,256,128]{3,2,1,0:T(8,128)S(1)}, f32[2,2,256,128]{3,2,1,0:T(8,128)S(1)}, u32[]{:S(2)}, u32[]{:S(2)}) collective-permute-start(f32[2,2,256,128]{3,2,1,0:T(8,128)S(1)} %get-tuple-element.39), channel_id=1, source_target_pairs={{0,1},{2,3},{4,5},{6,7},{1,0},{3,2},{5,4},{7,6},{8,9},{10,11},{12,... | collective-permute-start | bytes 1572872 | tf_op jit(solution)/shard_map/ppermute | solution.py:353
  10.4 19.2 %collective-permute-start.4 = (f32[2,2,256,128]{3,2,1,0:T(8,128)S(1)}, f32[2,2,256,128]{3,2,1,0:T(8,128)S(1)}, u32[]{:S(2)}, u32[]{:S(2)}) collective-permute-start(f32[2,2,256,128]{3,2,1,0:T(8,128)S(1)} %get-tuple-element.40), channel_id=1, source_target_pairs={{1,2},{3,4},{5,6},{2,1},{4,3},{6,5},{9,10},{11,12},{13,14},{10,9},... | collective-permute-start | bytes 1572872 | tf_op jit(solution)/shard_map/ppermute | solution.py:353
  12.8 9.9 %collective-permute-start.2 = (f32[2,128,256]{2,1,0:T(8,128)S(1)}, f32[2,128,256]{2,1,0:T(8,128)S(1)}, u32[]{:S(2)}, u32[]{:S(2)}) collective-permute-start(f32[2,128,256]{2,1,0:T(8,128)S(1)} %collective-permute-done.1), channel_id=1, source_target_pairs={{24,16},{0,8},{8,24},{16,0},{25,17},{1,9},{9,25},{17,1},{26,18},{2... | collective-permute-start | bytes 786440 | tf_op jit(solution)/shard_map/ppermute | solution.py:379
  18.4 6.1 %collective-permute-start.9 = (f32[2,2,128,128]{3,2,1,0:T(8,128)S(1)}, f32[2,2,128,128]{3,2,1,0:T(8,128)S(1)}, u32[]{:S(2)}, u32[]{:S(2)}) collective-permute-start(f32[2,2,128,128]{3,2,1,0:T(8,128)S(1)} %get-tuple-element.45), channel_id=1, source_target_pairs={{0,1},{2,3},{4,5},{6,7},{1,0},{3,2},{5,4},{7,6},{8,9},{10,11},{12,... | collective-permute-start | bytes 786440 | tf_op jit(solution)/shard_map/ppermute | solution.py:353
  20.7 8.8 %collective-permute-start.10 = (f32[2,2,128,128]{3,2,1,0:T(8,128)S(1)}, f32[2,2,128,128]{3,2,1,0:T(8,128)S(1)}, u32[]{:S(2)}, u32[]{:S(2)}) collective-permute-start(f32[2,2,128,128]{3,2,1,0:T(8,128)S(1)} %get-tuple-element.46), channel_id=1, source_target_pairs={{1,2},{3,4},{5,6},{2,1},{4,3},{6,5},{9,10},{11,12},{13,14},{10,9},... | collective-permute-start | bytes 786440 | tf_op jit(solution)/shard_map/ppermute | solution.py:353
  22.8 10.5 %collective-permute-start.5 = (f32[2,2,128,128]{3,2,1,0:T(8,128)S(1)}, f32[2,2,128,128]{3,2,1,0:T(8,128)S(1)}, u32[]{:S(2)}, u32[]{:S(2)}) collective-permute-start(f32[2,2,128,128]{3,2,1,0:T(8,128)S(1)} %get-tuple-element.41), channel_id=1, source_target_pairs={{0,1},{2,3},{4,5},{6,7},{1,0},{3,2},{5,4},{7,6},{8,9},{10,11},{12,... | collective-permute-start | bytes 786440 | tf_op jit(solution)/shard_map/ppermute | solution.py:353
  24.5 8.8 %collective-permute-start.6 = (f32[2,2,128,128]{3,2,1,0:T(8,128)S(1)}, f32[2,2,128,128]{3,2,1,0:T(8,128)S(1)}, u32[]{:S(2)}, u32[]{:S(2)}) collective-permute-start(f32[2,2,128,128]{3,2,1,0:T(8,128)S(1)} %get-tuple-element.42), channel_id=1, source_target_pairs={{1,2},{3,4},{5,6},{2,1},{4,3},{6,5},{9,10},{11,12},{13,14},{10,9},... | collective-permute-start | bytes 786440 | tf_op jit(solution)/shard_map/ppermute | solution.py:353
  41.5 7.4 %collective-permute-start.13 = (f32[2,2,128,128]{3,2,1,0:T(8,128)S(1)}, f32[2,2,128,128]{3,2,1,0:T(8,128)S(1)}, u32[]{:S(2)}, u32[]{:S(2)}) collective-permute-start(f32[2,2,128,128]{3,2,1,0:T(8,128)S(1)} %get-tuple-element.56), channel_id=1, source_target_pairs={{0,1},{2,3},{4,5},{6,7},{1,0},{3,2},{5,4},{7,6},{8,9},{10,11},{12,... | collective-permute-start | bytes 786440 | tf_op jit(solution)/shard_map/ppermute | solution.py:353
  43.2 7.8 %collective-permute-start.14 = (f32[2,2,128,128]{3,2,1,0:T(8,128)S(1)}, f32[2,2,128,128]{3,2,1,0:T(8,128)S(1)}, u32[]{:S(2)}, u32[]{:S(2)}) collective-permute-start(f32[2,2,128,128]{3,2,1,0:T(8,128)S(1)} %get-tuple-element.57), channel_id=1, source_target_pairs={{1,2},{3,4},{5,6},{2,1},{4,3},{6,5},{9,10},{11,12},{13,14},{10,9},... | collective-permute-start | bytes 786440 | tf_op jit(solution)/shard_map/ppermute | solution.py:353
  45.2 10.3 %collective-permute-start.19 = (f32[2,2,128,128]{3,2,1,0:T(8,128)S(1)}, f32[2,2,128,128]{3,2,1,0:T(8,128)S(1)}, u32[]{:S(2)}, u32[]{:S(2)}) collective-permute-start(f32[2,2,128,128]{3,2,1,0:T(8,128)S(1)} %get-tuple-element.62), channel_id=1, source_target_pairs={{0,1},{2,3},{4,5},{6,7},{1,0},{3,2},{5,4},{7,6},{8,9},{10,11},{12,... | collective-permute-start | bytes 786440 | tf_op jit(solution)/shard_map/ppermute | solution.py:353
  45.3 10.2 %collective-permute-start.20 = (f32[2,2,128,128]{3,2,1,0:T(8,128)S(1)}, f32[2,2,128,128]{3,2,1,0:T(8,128)S(1)}, u32[]{:S(2)}, u32[]{:S(2)}) collective-permute-start(f32[2,2,128,128]{3,2,1,0:T(8,128)S(1)} %get-tuple-element.63), channel_id=1, source_target_pairs={{1,2},{3,4},{5,6},{2,1},{4,3},{6,5},{9,10},{11,12},{13,14},{10,9},... | collective-permute-start | bytes 786440 | tf_op jit(solution)/shard_map/ppermute | solution.py:353
  48.8 23.0 %collective-permute-start.11 = (f32[2,2,256,128]{3,2,1,0:T(8,128)S(1)}, f32[2,2,256,128]{3,2,1,0:T(8,128)S(1)}, u32[]{:S(2)}, u32[]{:S(2)}) collective-permute-start(f32[2,2,256,128]{3,2,1,0:T(8,128)S(1)} %get-tuple-element.53), channel_id=1, source_target_pairs={{0,1},{2,3},{4,5},{6,7},{1,0},{3,2},{5,4},{7,6},{8,9},{10,11},{12,... | collective-permute-start | bytes 1572872 | tf_op jit(solution)/shard_map/ppermute | solution.py:353
  48.9 22.9 %collective-permute-start.12 = (f32[2,2,256,128]{3,2,1,0:T(8,128)S(1)}, f32[2,2,256,128]{3,2,1,0:T(8,128)S(1)}, u32[]{:S(2)}, u32[]{:S(2)}) collective-permute-start(f32[2,2,256,128]{3,2,1,0:T(8,128)S(1)} %get-tuple-element.54), channel_id=1, source_target_pairs={{1,2},{3,4},{5,6},{2,1},{4,3},{6,5},{9,10},{11,12},{13,14},{10,9},... | collective-permute-start | bytes 1572872 | tf_op jit(solution)/shard_map/ppermute | solution.py:353
  51.1 8.6 %collective-permute-start.16 = (f32[1,128,256]{2,1,0:T(8,128)S(1)}, f32[1,128,256]{2,1,0:T(8,128)S(1)}, u32[]{:S(2)}, u32[]{:S(2)}) collective-permute-start(f32[1,128,256]{2,1,0:T(8,128)S(1)} %get-tuple-element.59), channel_id=1, source_target_pairs={{8,24},{16,0},{9,25},{17,1},{10,26},{18,2},{11,27},{19,3},{12,28},... | collective-permute-start | bytes 393224 | tf_op jit(solution)/shard_map/ppermute | solution.py:379
  55.6 9.2 %collective-permute-start.21 = (f32[2,128,256]{2,1,0:T(8,128)S(1)}, f32[2,128,256]{2,1,0:T(8,128)S(1)}, u32[]{:S(2)}, u32[]{:S(2)}) collective-permute-start(f32[2,128,256]{2,1,0:T(8,128)S(1)} %get-tuple-element.64), channel_id=1, source_target_pairs={{0,8},{16,24},{8,0},{24,16},{1,9},{17,25},{9,1},{25,17},{2,10},{18... | collective-permute-start | bytes 786440 | tf_op jit(solution)/shard_map/ppermute | solution.py:353
  56.3 14.2 %collective-permute-start.22 = (f32[2,128,256]{2,1,0:T(8,128)S(1)}, f32[2,128,256]{2,1,0:T(8,128)S(1)}, u32[]{:S(2)}, u32[]{:S(2)}) collective-permute-start(f32[2,128,256]{2,1,0:T(8,128)S(1)} %get-tuple-element.65), channel_id=1, source_target_pairs={{8,16},{16,8},{9,17},{17,9},{10,18},{18,10},{11,19},{19,11},{12,20... | collective-permute-start | bytes 786440 | tf_op jit(solution)/shard_map/ppermute | solution.py:353
  59.7 14.6 %collective-permute-start.18 = (f32[2,128,256]{2,1,0:T(8,128)S(1)}, f32[2,128,256]{2,1,0:T(8,128)S(1)}, u32[]{:S(2)}, u32[]{:S(2)}) collective-permute-start(f32[2,128,256]{2,1,0:T(8,128)S(1)} %get-tuple-element.60), channel_id=1, source_target_pairs={{0,8},{16,24},{8,0},{24,16},{1,9},{17,25},{9,1},{25,17},{2,10},{18... | collective-permute-start | bytes 786440 | tf_op jit(solution)/shard_map/ppermute | solution.py:353
  64.8 13.5 %collective-permute-start.15 = (f32[1,128,256]{2,1,0:T(8,128)S(1)}, f32[1,128,256]{2,1,0:T(8,128)S(1)}, u32[]{:S(2)}, u32[]{:S(2)}) collective-permute-start(f32[1,128,256]{2,1,0:T(8,128)S(1)} %get-tuple-element.58), channel_id=1, source_target_pairs={{8,16},{16,8},{9,17},{17,9},{10,18},{18,10},{11,19},{19,11},{12,20... | collective-permute-start | bytes 393224 | tf_op jit(solution)/shard_map/ppermute | solution.py:353
  70.5 7.8 %collective-permute-start.17 = (f32[1,128,256]{2,1,0:T(8,128)S(1)}, f32[1,128,256]{2,1,0:T(8,128)S(1)}, u32[]{:S(2)}, u32[]{:S(2)}) collective-permute-start(f32[1,128,256]{2,1,0:T(8,128)S(1)} %collective-permute-done.16), channel_id=1, source_target_pairs={{24,16},{0,8},{25,17},{1,9},{26,18},{2,10},{27,19},{3,11},{28,20},... | collective-permute-start | bytes 393224 | tf_op jit(solution)/shard_map/ppermute | solution.py:379
  (6 other events, 54.4 us)

commit v2 on v1

--- a/solution.py
+++ b/solution.py
@@ -90,11 +90,13 @@
 
 def places_of(margin, high, wide):
     row_at, col_at = lax.axis_index("row"), lax.axis_index("col")
-    last = lax.axis_size("row") - 1
     row_e = jnp.where(row_at % 2 == 0, margin + high, 0)
     col_e = jnp.where(col_at % 2 == 0, margin + wide, 0)
-    partnered = (row_at > 0) & ((row_at < last) | (last % 2 == 0))
-    return row_e, margin + high - row_e, col_e, margin + wide - col_e, partnered
+    partnered = []
+    for axis, at in (("row", row_at), ("col", col_at)):
+        last = lax.axis_size(axis) - 1
+        partnered.append((at > 0) & ((at < last) | (last % 2 == 0)))
+    return row_e, margin + high - row_e, col_e, margin + wide - col_e, *partnered
 
 
 def halves(places, first, margin):
@@ -104,6 +106,10 @@
 def inner_halves(places, first, margin):
     at = [jnp.maximum(places[first + k] - 2 * margin, 0) for k in range(2)]
     return [pl.ds(pl.multiple_of(start, 128), margin) for start in at]
+
+
+def kept(value, odd, partnered):
+    return jnp.where(partnered, value, 0.0) if odd else value
 
 
 def hand_out(gext, corners, sides, middle):
@@ -114,8 +120,8 @@
     for part in range(2):
         for k in range(2):
             for j in range(2):
-                corners[k][j, part] = gext[part, outer_rows[j], outer_cols[k]]
-            sides[k][part] = gext[part, inner_rows, outer_cols[k]]
+                corners[k][j, part] = kept(gext[part, outer_rows[j], outer_cols[k]], k, places[5])
+            sides[k][part] = kept(gext[part, inner_rows, outer_cols[k]], k, places[5])
         middle[part] = gext[part, :, inner_cols]
 
 
@@ -268,9 +274,8 @@
             strip[...] = middle[part, at, :]
             for k in range(2):
                 strip[:, cols[k]] += corners[k][int(at is rows[1]), part]
-    if len(strips_o) == 2:
-        relayed = strips_o[1]
-        relayed[...] = jnp.where(places[4], relayed[...], 0.0)
+    for strip in strips_o:
+        strip[...] = kept(strip[...], 1, places[4])
 
 
 def half(strips, part):
@@ -311,18 +316,19 @@
     for which, outs in enumerate(((row_e0, row_o0), (row_e1, row_o1))):
         for part in range(2):
             for k in range(2):
-                outs[k][part] = tile[which, part, rows[k], :]
-                (side_e, side_o)[k][which, part] = tile[which, part, :, cols[k]]
-    row_o1[...] = jnp.where(places[4], row_o1[...], 0.0)
+                outs[k][part] = kept(tile[which, part, rows[k], :], k, places[4])
+                side = kept(tile[which, part, :, cols[k]], k, places[5])
+                (side_e, side_o)[k][which, part] = side
 
 
 def cut_kernel(halo_e, halo_o, to_even, to_odd):
     margin = to_even.shape[2]
-    cols = inner_halves(places_of(margin, 0, halo_e.shape[2]), 2, margin)
+    places = places_of(margin, 0, halo_e.shape[2])
+    cols = inner_halves(places, 2, margin)
     for j, halo in enumerate((halo_e, halo_o)):
         for part in range(2):
             to_even[j, part] = halo[part, :, cols[0]]
-            to_odd[j, part] = halo[part, :, cols[1]]
+            to_odd[j, part] = kept(halo[part, :, cols[1]], 1, places[5])
 
 
 def turn_kernel(offsets, live, phase, table, light, slots_at, kernel, left, probe):
@@ -347,10 +353,28 @@
     return [(low, low + 1) for low in range(1, count - 1, 2)]
 
 
+def lonely(count):
+    paired = {at for pair in odd_pairs(count) for at in pair}
+    return [at for at in range(count) if at not in paired]
+
+
 def swap(axis, value, odd):
-    count = lax.axis_size(axis)
-    pairs = odd_pairs(count) if odd else even_pairs(count)
-    return lax.ppermute(value, axis, pairs + [(high, low) for low, high in pairs])
+    rows, cols = lax.axis_size("row"), lax.axis_size("col")
+    pairs = []
+    if axis == "row":
+        for low, high in odd_pairs(rows) if odd else even_pairs(rows):
+            pairs += [((low, col), (high, col)) for col in range(cols)]
+        for row in lonely(rows) if odd else ():
+            pairs += [((row, low), (row, high)) for low, high in even_pairs(cols)]
+    else:
+        for low, high in odd_pairs(cols) if odd else even_pairs(cols):
+            pairs += [((row, low), (row, high)) for row in range(rows)]
+        step = 2 if rows % 4 == 0 else 1
+        across = [row for row in range(rows - step) if row // step % 2 == 0]
+        for col in lonely(cols) if odd else ():
+            pairs += [((row, col), (row + step, col)) for row in across]
+    flat = [tuple(row * cols + col for row, col in pair) for pair in pairs]
+    return lax.ppermute(value, ("row", "col"), flat + [(b, a) for a, b in flat])
 
 
 def closed(steps, spare):

time: 79.6 us -> 74.6 us (0.937)
  the two profiles are of different devices: /device:TPU:10 before, /device:TPU:11 now
where the time goes in v2:
time: 74.6 us; the launch traced here: 74.4 us
  starting transfers between devices  30.3 us (41%)
  waiting for transfers between devices  23.8 us (32%)
  Pallas kernels  17.6 us (24%)
  between operations  1.53 us (2%)
  local copies, waits for them, and re-layouts  1.25 us (2%)
    ppermute x19, starting transfers between devices, swap(): return lax.ppermute(value, ('row', 'col'), flat + [(b, a) for a, b in flat])  22.6 us
    ppermute x19, waiting for transfers between devices, swap(): return lax.ppermute(value, ('row', 'col'), flat + [(b, a) for a, b in flat])  19.9 us
    ppermute x4, starting transfers between devices, relay(): return lax.ppermute(value, axis, steps)  7.71 us
    pallas_call x1, Pallas kernels, per_device(): call(exit_kernel, out_shape=(field, *pieces), in_specs=[VMEM] * 11, out_s...  4.42 us
    ppermute x4, waiting for transfers between devices, relay(): return lax.ppermute(value, axis, steps)  3.86 us
    pallas_call x1, Pallas kernels, per_device(): call(near_kernel, out_shape=field, in_specs=[VMEM] * 11, out_specs=VMEM,...  3.71 us
    pallas_call x1, Pallas kernels, per_device(): call(first_kernel, out_shape=(*pieces[:2], sides, sides, pieces[4]), in_s...  3.71 us
    pallas_call x3, Pallas kernels, per_device(): pl.pallas_call(functools.partial(final_kernel, steps), out_shape=(whole,...  2.86 us
  transfers between devices with their start and end apart: 23, of which 9 were waited for; matrix products, arithmetic and copies ran while one was open for 0% of the time, Pallas kernels for 11%

profile of v2, /device:TPU:11, one launch (start us, length us, event | category | flops | bytes accessed | tf_op | source)
XLA Modules:
  0.0 74.4 jit_solution(10556826365184529909)
XLA Ops:
  0.6 1.2 %copy-done = f32[2,2,256,256]{3,2,1,0:T(8,128)S(1)} copy-done((f32[2,2,256,256]{3,2,1,0:T(8,128)S(1)}, f32[2,2,256,256]{3,2,1,0:T(8,128)}, u32[]{:S(2)}) %copy-start) | copy-done | bytes 1048600
  2.1 1.3 %collective-permute-start.1 = (f32[2,128,256]{2,1,0:T(8,128)S(1)}, f32[2,128,256]{2,1,0:T(8,128)S(1)}, u32[]{:S(2)}, u32[]{:S(2)}) collective-permute-start(f32[2,128,256]{2,1,0:T(8,128)S(1)} %get-tuple-element.38), channel_id=1, source_target_pairs={{8,24},{16,0},{24,8},{0,16},{9,25},{17,1},{25,9},{1,17},{10,26},{1... | collective-permute-start | bytes 786440 | tf_op jit(solution)/shard_map/ppermute | solution.py:403
  3.6 1.2 %collective-permute-start.8 = (f32[2,128,256]{2,1,0:T(8,128)S(1)}, f32[2,128,256]{2,1,0:T(8,128)S(1)}, u32[]{:S(2)}, u32[]{:S(2)}) collective-permute-start(f32[2,128,256]{2,1,0:T(8,128)S(1)} %get-tuple-element.44), channel_id=1, source_target_pairs={{8,16},{9,17},{10,18},{11,19},{12,20},{13,21},{14,22},{15,23},{0,1... | collective-permute-start | bytes 786440 | tf_op jit(solution)/shard_map/ppermute | solution.py:377
  4.8 1.3 %collective-permute-start = (f32[2,128,256]{2,1,0:T(8,128)S(1)}, f32[2,128,256]{2,1,0:T(8,128)S(1)}, u32[]{:S(2)}, u32[]{:S(2)}) collective-permute-start(f32[2,128,256]{2,1,0:T(8,128)S(1)} %get-tuple-element.37), channel_id=1, source_target_pairs={{0,8},{1,9},{2,10},{3,11},{4,12},{5,13},{6,14},{7,15},{16,24},{17,... | collective-permute-start | bytes 786440 | tf_op jit(solution)/shard_map/ppermute | solution.py:377
  6.4 3.0 %collective-permute-done.1 = f32[2,128,256]{2,1,0:T(8,128)S(1)} collective-permute-done((f32[2,128,256]{2,1,0:T(8,128)S(1)}, f32[2,128,256]{2,1,0:T(8,128)S(1)}, u32[]{:S(2)}, u32[]{:S(2)}) %collective-permute-start.1) | collective-permute-done | bytes 262176 | tf_op jit(solution)/shard_map/ppermute | solution.py:403
  9.3 2.9 %collective-permute-start.4 = (f32[2,2,256,128]{3,2,1,0:T(8,128)S(1)}, f32[2,2,256,128]{3,2,1,0:T(8,128)S(1)}, u32[]{:S(2)}, u32[]{:S(2)}) collective-permute-start(f32[2,2,256,128]{3,2,1,0:T(8,128)S(1)} %get-tuple-element.40), channel_id=1, source_target_pairs={{1,2},{9,10},{17,18},{25,26},{3,4},{11,12},{19,20},{27,28},{5,6},{... | collective-permute-start | bytes 1572872 | tf_op jit(solution)/shard_map/ppermute | solution.py:377
  13.3 2.6 %collective-permute-done.8.halo_o.row_o = f32[2,128,256]{2,1,0:T(8,128)S(1)} collective-permute-done((f32[2,128,256]{2,1,0:T(8,128)S(1)}, f32[2,128,256]{2,1,0:T(8,128)S(1)}, u32[]{:S(2)}, u32[]{:S(2)}) %collective-permute-start.8) | collective-permute-done | bytes 262176 | tf_op jit(solution)/shard_map/ppermute | solution.py:377
  15.9 3.3 %collective-permute-start.9 = (f32[2,2,128,128]{3,2,1,0:T(8,128)S(1)}, f32[2,2,128,128]{3,2,1,0:T(8,128)S(1)}, u32[]{:S(2)}, u32[]{:S(2)}) collective-permute-start(f32[2,2,128,128]{3,2,1,0:T(8,128)S(1)} %get-tuple-element.45), channel_id=1, source_target_pairs={{0,1},{8,9},{16,17},{24,25},{2,3},{10,11},{18,19},{26,27},{4,5},{1... | collective-permute-start | bytes 786440 | tf_op jit(solution)/shard_map/ppermute | solution.py:377
  19.6 3.0 %collective-permute-start.10 = (f32[2,2,128,128]{3,2,1,0:T(8,128)S(1)}, f32[2,2,128,128]{3,2,1,0:T(8,128)S(1)}, u32[]{:S(2)}, u32[]{:S(2)}) collective-permute-start(f32[2,2,128,128]{3,2,1,0:T(8,128)S(1)} %get-tuple-element.46), channel_id=1, source_target_pairs={{1,2},{9,10},{17,18},{25,26},{3,4},{11,12},{19,20},{27,28},{5,6},{... | collective-permute-start | bytes 786440 | tf_op jit(solution)/shard_map/ppermute | solution.py:377
  23.4 1.3 %collective-permute-start.6 = (f32[2,2,128,128]{3,2,1,0:T(8,128)S(1)}, f32[2,2,128,128]{3,2,1,0:T(8,128)S(1)}, u32[]{:S(2)}, u32[]{:S(2)}) collective-permute-start(f32[2,2,128,128]{3,2,1,0:T(8,128)S(1)} %get-tuple-element.42), channel_id=1, source_target_pairs={{1,2},{9,10},{17,18},{25,26},{3,4},{11,12},{19,20},{27,28},{5,6},{... | collective-permute-start | bytes 786440 | tf_op jit(solution)/shard_map/ppermute | solution.py:377
  25.4 2.3 %turn.1 = (f32[8,128]{1,0:T(8,128)S(1)}, f32[2,256,256]{2,1,0:T(8,128)S(1)}, bf16[2,3,256,256]{3,2,1,0:T(8,128)(2,1)S(1)}, f32[2,256,256]{2,1,0:T(8,128)S(1)}) custom-call(s32[2,2]{1,0:T(2,128)S(1)} %copy-done.5, s32[1,1]{1,0:T(1,128)S(6)} %copy.17.live, f32[256,256]{1,0:T(8,128)S(1)} %copy-done.4, bf16[2,3,256,256]{3,2,1,0:T(8,128)(2,1)S(1)} %copy-done.2, ...), custom_call_target="tpu_custom_call" | custom-call | tf_op jit(solution)/shard_map/turn/pallas_call | solution.py:454
  27.8 3.7 %near.1 = f32[2,2,256,256]{3,2,1,0:T(8,128)S(1)} custom-call(f32[8,128]{1,0:T(8,128)S(1)} %get-tuple-element.36.slots_at, f32[2,2,256,256]{3,2,1,0:T(8,128)S(1)} %copy-done.1, f32[2,128,256]{2,1,0:T(8,128)S(1)} %collective-permute-done.7.halo_e.row_e, f32[2,128,256]{2,1,0:T(8,128)S(1)} %collective-permute-done.8.halo_o.row_o, ...), custom_call_target="tpu_custom_call" | custom-call | flops 2415919104 | bytes 8388608 | tf_op jit(solution)/shard_map/near/pallas_call | solution.py:477
  31.5 4.4 %exit.1 = (f32[2,2,256,256]{3,2,1,0:T(8,128)S(1)}, f32[2,2,128,128]{3,2,1,0:T(8,128)S(1)}, f32[2,2,128,128]{3,2,1,0:T(8,128)S(1)}, f32[2,256,128]{2,1,0:T(8,128)...) custom-call(f32[8,128]{1,0:T(8,128)S(1)} %get-tuple-element.36.slots_at, f32[2,2,256,256]{3,2,1,0:T(8,128)S(1)} %copy-done.1, ...), custom_call_target="tpu_custom_call" | custom-call | flops 2415919104 | bytes 8388608 | tf_op jit(solution)/shard_map/exit/pallas_call | solution.py:489
  35.9 3.7 %first.1 = (f32[2,2,128,128]{3,2,1,0:T(8,128)S(1)}, f32[2,2,128,128]{3,2,1,0:T(8,128)S(1)}, f32[2,2,256,128]{3,2,1,0:T(8,128)S(1)}, f32[2,2,256,128]{3,2,1,0:T(8,128)S(1)}, f32[2,512,256]{2,1,0:T(8,128)S(1)}) custom-call(f32[8,128]{1,0:T(8,128)S(1)} %get-tuple-element.36.slots_at, f32[2,2,256,256]{3,2,1,0:T(8,128)S(1)} %get-tuple-element.50.g_near, ...), custom_call_target="tpu_custom_call" | custom-call | flops 2415919104 | bytes 8388608 | tf_op jit(solution)/shard_map/first/pallas_call | solution.py:513
  41.4 1.6 %collective-permute-start.19 = (f32[2,2,128,128]{3,2,1,0:T(8,128)S(1)}, f32[2,2,128,128]{3,2,1,0:T(8,128)S(1)}, u32[]{:S(2)}, u32[]{:S(2)}) collective-permute-start(f32[2,2,128,128]{3,2,1,0:T(8,128)S(1)} %get-tuple-element.62), channel_id=1, source_target_pairs={{0,1},{8,9},{16,17},{24,25},{2,3},{10,11},{18,19},{26,27},{4,5},{1... | collective-permute-start | bytes 786440 | tf_op jit(solution)/shard_map/ppermute | solution.py:377
  43.4 1.4 %collective-permute-start.12 = (f32[2,2,256,128]{3,2,1,0:T(8,128)S(1)}, f32[2,2,256,128]{3,2,1,0:T(8,128)S(1)}, u32[]{:S(2)}, u32[]{:S(2)}) collective-permute-start(f32[2,2,256,128]{3,2,1,0:T(8,128)S(1)} %get-tuple-element.54), channel_id=1, source_target_pairs={{1,2},{9,10},{17,18},{25,26},{3,4},{11,12},{19,20},{27,28},{5,6},{... | collective-permute-start | bytes 1572872 | tf_op jit(solution)/shard_map/ppermute | solution.py:377
  44.8 1.7 %collective-permute-done.14.corner_o = f32[2,2,128,128]{3,2,1,0:T(8,128)S(1)} collective-permute-done((f32[2,2,128,128]{3,2,1,0:T(8,128)S(1)}, f32[2,2,128,128]{3,2,1,0:T(8,128)S(1)}, u32[]{:S(2)}, u32[]{:S(2)}) %collective-permute-start.14) | collective-permute-done | bytes 262176 | tf_op jit(solution)/shard_map/ppermute | solution.py:377
  46.6 4.1 %collective-permute-start.16 = (f32[1,128,256]{2,1,0:T(8,128)S(1)}, f32[1,128,256]{2,1,0:T(8,128)S(1)}, u32[]{:S(2)}, u32[]{:S(2)}) collective-permute-start(f32[1,128,256]{2,1,0:T(8,128)S(1)} %get-tuple-element.59), channel_id=1, source_target_pairs={{8,24},{16,0},{9,25},{17,1},{10,26},{18,2},{11,27},{19,3},{12,28},... | collective-permute-start | bytes 393224 | tf_op jit(solution)/shard_map/ppermute | solution.py:403
  51.0 1.9 %collective-permute-start.22 = (f32[2,128,256]{2,1,0:T(8,128)S(1)}, f32[2,128,256]{2,1,0:T(8,128)S(1)}, u32[]{:S(2)}, u32[]{:S(2)}) collective-permute-start(f32[2,128,256]{2,1,0:T(8,128)S(1)} %get-tuple-element.65), channel_id=1, source_target_pairs={{8,16},{9,17},{10,18},{11,19},{12,20},{13,21},{14,22},{15,23},{0,1... | collective-permute-start | bytes 786440 | tf_op jit(solution)/shard_map/ppermute | solution.py:377
  54.7 4.0 %collective-permute-done.21.refs_1_ = f32[2,128,256]{2,1,0:T(8,128)S(1)} collective-permute-done((f32[2,128,256]{2,1,0:T(8,128)S(1)}, f32[2,128,256]{2,1,0:T(8,128)S(1)}, u32[]{:S(2)}, u32[]{:S(2)}) %collective-permute-start.21) | collective-permute-done | bytes 262176 | tf_op jit(solution)/shard_map/ppermute | solution.py:377
  59.0 6.1 %collective-permute-done.22.refs_2_ = f32[2,128,256]{2,1,0:T(8,128)S(1)} collective-permute-done((f32[2,128,256]{2,1,0:T(8,128)S(1)}, f32[2,128,256]{2,1,0:T(8,128)S(1)}, u32[]{:S(2)}, u32[]{:S(2)}) %collective-permute-start.22) | collective-permute-done | bytes 262176 | tf_op jit(solution)/shard_map/ppermute | solution.py:377
  65.1 1.3 %collective-permute-start.17 = (f32[1,128,256]{2,1,0:T(8,128)S(1)}, f32[1,128,256]{2,1,0:T(8,128)S(1)}, u32[]{:S(2)}, u32[]{:S(2)}) collective-permute-start(f32[1,128,256]{2,1,0:T(8,128)S(1)} %collective-permute-done.16), channel_id=1, source_target_pairs={{24,16},{0,8},{25,17},{1,9},{26,18},{2,10},{27,19},{3,11},{28,20},... | collective-permute-start | bytes 393224 | tf_op jit(solution)/shard_map/ppermute | solution.py:403
  66.4 1.1 %shard_map.86 = (f32[2,2,256,256]{3,2,1,0:T(8,128)}, f32[2,2,256,256]{3,2,1,0:T(8,128)}) custom-call(f32[2,2,256,256]{3,2,1,0:T(8,128)S(1)} %copy-done.1, f32[2,2,256,128]{3,2,1,0:T(8,128)S(1)} %collective-permute-done.11.side_e, f32[2,2,256,128]{3,2,1,0:T(8,128)S(1)} %collective-permute-done.12.side_o, f32[2,512,256]{2,1,0:T(8,128)S(1)} %get-tuple-element.61.middle.refs_0_, ...), custom_call_target="tpu_custom_call" | custom-call | tf_op jit(solution)/shard_map/pallas_call | solution.py:544
  68.8 4.7 %collective-permute-done.15.refs_1_ = f32[1,128,256]{2,1,0:T(8,128)S(1)} collective-permute-done((f32[1,128,256]{2,1,0:T(8,128)S(1)}, f32[1,128,256]{2,1,0:T(8,128)S(1)}, u32[]{:S(2)}, u32[]{:S(2)}) %collective-permute-start.15) | collective-permute-done | bytes 131104 | tf_op jit(solution)/shard_map/ppermute | solution.py:377
  (48 shorter events, 9.9 us)
Async XLA Ops:
  1.9 23.5 %copy-start.3 = (f32[2,256,256]{2,1,0:T(8,128)S(1)}, f32[2,256,256]{2,1,0:T(8,128)}, u32[]{:S(2)}) copy-start(f32[2,256,256]{2,1,0:T(8,128)} %light.1) | copy-start | bytes 1572868
  2.1 7.3 %collective-permute-start.1 = (f32[2,128,256]{2,1,0:T(8,128)S(1)}, f32[2,128,256]{2,1,0:T(8,128)S(1)}, u32[]{:S(2)}, u32[]{:S(2)}) collective-permute-start(f32[2,128,256]{2,1,0:T(8,128)S(1)} %get-tuple-element.38), channel_id=1, source_target_pairs={{8,24},{16,0},{24,8},{0,16},{9,25},{17,1},{25,9},{1,17},{10,26},{1... | collective-permute-start | bytes 786440 | tf_op jit(solution)/shard_map/ppermute | solution.py:403
  3.4 8.9 %collective-permute-start.7 = (f32[2,128,256]{2,1,0:T(8,128)S(1)}, f32[2,128,256]{2,1,0:T(8,128)S(1)}, u32[]{:S(2)}, u32[]{:S(2)}) collective-permute-start(f32[2,128,256]{2,1,0:T(8,128)S(1)} %get-tuple-element.43), channel_id=1, source_target_pairs={{0,8},{1,9},{2,10},{3,11},{4,12},{5,13},{6,14},{7,15},{16,24},{17,... | collective-permute-start | bytes 786440 | tf_op jit(solution)/shard_map/ppermute | solution.py:377
  3.6 12.2 %collective-permute-start.8 = (f32[2,128,256]{2,1,0:T(8,128)S(1)}, f32[2,128,256]{2,1,0:T(8,128)S(1)}, u32[]{:S(2)}, u32[]{:S(2)}) collective-permute-start(f32[2,128,256]{2,1,0:T(8,128)S(1)} %get-tuple-element.44), channel_id=1, source_target_pairs={{8,16},{9,17},{10,18},{11,19},{12,20},{13,21},{14,22},{15,23},{0,1... | collective-permute-start | bytes 786440 | tf_op jit(solution)/shard_map/ppermute | solution.py:377
  4.8 14.8 %collective-permute-start = (f32[2,128,256]{2,1,0:T(8,128)S(1)}, f32[2,128,256]{2,1,0:T(8,128)S(1)}, u32[]{:S(2)}, u32[]{:S(2)}) collective-permute-start(f32[2,128,256]{2,1,0:T(8,128)S(1)} %get-tuple-element.37), channel_id=1, source_target_pairs={{0,8},{1,9},{2,10},{3,11},{4,12},{5,13},{6,14},{7,15},{16,24},{17,... | collective-permute-start | bytes 786440 | tf_op jit(solution)/shard_map/ppermute | solution.py:377
  6.1 21.6 %collective-permute-start.3 = (f32[2,2,256,128]{3,2,1,0:T(8,128)S(1)}, f32[2,2,256,128]{3,2,1,0:T(8,128)S(1)}, u32[]{:S(2)}, u32[]{:S(2)}) collective-permute-start(f32[2,2,256,128]{3,2,1,0:T(8,128)S(1)} %get-tuple-element.39), channel_id=1, source_target_pairs={{0,1},{8,9},{16,17},{24,25},{2,3},{10,11},{18,19},{26,27},{4,5},{1... | collective-permute-start | bytes 1572872 | tf_op jit(solution)/shard_map/ppermute | solution.py:377
  9.3 18.4 %collective-permute-start.4 = (f32[2,2,256,128]{3,2,1,0:T(8,128)S(1)}, f32[2,2,256,128]{3,2,1,0:T(8,128)S(1)}, u32[]{:S(2)}, u32[]{:S(2)}) collective-permute-start(f32[2,2,256,128]{3,2,1,0:T(8,128)S(1)} %get-tuple-element.40), channel_id=1, source_target_pairs={{1,2},{9,10},{17,18},{25,26},{3,4},{11,12},{19,20},{27,28},{5,6},{... | collective-permute-start | bytes 1572872 | tf_op jit(solution)/shard_map/ppermute | solution.py:377
  12.3 10.3 %collective-permute-start.2 = (f32[2,128,256]{2,1,0:T(8,128)S(1)}, f32[2,128,256]{2,1,0:T(8,128)S(1)}, u32[]{:S(2)}, u32[]{:S(2)}) collective-permute-start(f32[2,128,256]{2,1,0:T(8,128)S(1)} %collective-permute-done.1), channel_id=1, source_target_pairs={{24,16},{0,8},{8,24},{16,0},{25,17},{1,9},{9,25},{17,1},{26,18},{2... | collective-permute-start | bytes 786440 | tf_op jit(solution)/shard_map/ppermute | solution.py:403
  15.9 7.6 %collective-permute-start.9 = (f32[2,2,128,128]{3,2,1,0:T(8,128)S(1)}, f32[2,2,128,128]{3,2,1,0:T(8,128)S(1)}, u32[]{:S(2)}, u32[]{:S(2)}) collective-permute-start(f32[2,2,128,128]{3,2,1,0:T(8,128)S(1)} %get-tuple-element.45), channel_id=1, source_target_pairs={{0,1},{8,9},{16,17},{24,25},{2,3},{10,11},{18,19},{26,27},{4,5},{1... | collective-permute-start | bytes 786440 | tf_op jit(solution)/shard_map/ppermute | solution.py:377
  19.6 8.1 %collective-permute-start.10 = (f32[2,2,128,128]{3,2,1,0:T(8,128)S(1)}, f32[2,2,128,128]{3,2,1,0:T(8,128)S(1)}, u32[]{:S(2)}, u32[]{:S(2)}) collective-permute-start(f32[2,2,128,128]{3,2,1,0:T(8,128)S(1)} %get-tuple-element.46), channel_id=1, source_target_pairs={{1,2},{9,10},{17,18},{25,26},{3,4},{11,12},{19,20},{27,28},{5,6},{... | collective-permute-start | bytes 786440 | tf_op jit(solution)/shard_map/ppermute | solution.py:377
  22.6 8.9 %collective-permute-start.5 = (f32[2,2,128,128]{3,2,1,0:T(8,128)S(1)}, f32[2,2,128,128]{3,2,1,0:T(8,128)S(1)}, u32[]{:S(2)}, u32[]{:S(2)}) collective-permute-start(f32[2,2,128,128]{3,2,1,0:T(8,128)S(1)} %get-tuple-element.41), channel_id=1, source_target_pairs={{0,1},{8,9},{16,17},{24,25},{2,3},{10,11},{18,19},{26,27},{4,5},{1... | collective-permute-start | bytes 786440 | tf_op jit(solution)/shard_map/ppermute | solution.py:377
  23.4 8.0 %collective-permute-start.6 = (f32[2,2,128,128]{3,2,1,0:T(8,128)S(1)}, f32[2,2,128,128]{3,2,1,0:T(8,128)S(1)}, u32[]{:S(2)}, u32[]{:S(2)}) collective-permute-start(f32[2,2,128,128]{3,2,1,0:T(8,128)S(1)} %get-tuple-element.42), channel_id=1, source_target_pairs={{1,2},{9,10},{17,18},{25,26},{3,4},{11,12},{19,20},{27,28},{5,6},{... | collective-permute-start | bytes 786440 | tf_op jit(solution)/shard_map/ppermute | solution.py:377
  39.6 3.7 %collective-permute-start.13 = (f32[2,2,128,128]{3,2,1,0:T(8,128)S(1)}, f32[2,2,128,128]{3,2,1,0:T(8,128)S(1)}, u32[]{:S(2)}, u32[]{:S(2)}) collective-permute-start(f32[2,2,128,128]{3,2,1,0:T(8,128)S(1)} %get-tuple-element.56), channel_id=1, source_target_pairs={{0,1},{8,9},{16,17},{24,25},{2,3},{10,11},{18,19},{26,27},{4,5},{1... | collective-permute-start | bytes 786440 | tf_op jit(solution)/shard_map/ppermute | solution.py:377
  40.4 6.1 %collective-permute-start.14 = (f32[2,2,128,128]{3,2,1,0:T(8,128)S(1)}, f32[2,2,128,128]{3,2,1,0:T(8,128)S(1)}, u32[]{:S(2)}, u32[]{:S(2)}) collective-permute-start(f32[2,2,128,128]{3,2,1,0:T(8,128)S(1)} %get-tuple-element.57), channel_id=1, source_target_pairs={{1,2},{9,10},{17,18},{25,26},{3,4},{11,12},{19,20},{27,28},{5,6},{... | collective-permute-start | bytes 786440 | tf_op jit(solution)/shard_map/ppermute | solution.py:377
  41.4 9.3 %collective-permute-start.19 = (f32[2,2,128,128]{3,2,1,0:T(8,128)S(1)}, f32[2,2,128,128]{3,2,1,0:T(8,128)S(1)}, u32[]{:S(2)}, u32[]{:S(2)}) collective-permute-start(f32[2,2,128,128]{3,2,1,0:T(8,128)S(1)} %get-tuple-element.62), channel_id=1, source_target_pairs={{0,1},{8,9},{16,17},{24,25},{2,3},{10,11},{18,19},{26,27},{4,5},{1... | collective-permute-start | bytes 786440 | tf_op jit(solution)/shard_map/ppermute | solution.py:377
  43.0 7.8 %collective-permute-start.20 = (f32[2,2,128,128]{3,2,1,0:T(8,128)S(1)}, f32[2,2,128,128]{3,2,1,0:T(8,128)S(1)}, u32[]{:S(2)}, u32[]{:S(2)}) collective-permute-start(f32[2,2,128,128]{3,2,1,0:T(8,128)S(1)} %get-tuple-element.63), channel_id=1, source_target_pairs={{1,2},{9,10},{17,18},{25,26},{3,4},{11,12},{19,20},{27,28},{5,6},{... | collective-permute-start | bytes 786440 | tf_op jit(solution)/shard_map/ppermute | solution.py:377
  43.0 23.4 %collective-permute-start.11 = (f32[2,2,256,128]{3,2,1,0:T(8,128)S(1)}, f32[2,2,256,128]{3,2,1,0:T(8,128)S(1)}, u32[]{:S(2)}, u32[]{:S(2)}) collective-permute-start(f32[2,2,256,128]{3,2,1,0:T(8,128)S(1)} %get-tuple-element.53), channel_id=1, source_target_pairs={{0,1},{8,9},{16,17},{24,25},{2,3},{10,11},{18,19},{26,27},{4,5},{1... | collective-permute-start | bytes 1572872 | tf_op jit(solution)/shard_map/ppermute | solution.py:377
  43.4 23.0 %collective-permute-start.12 = (f32[2,2,256,128]{3,2,1,0:T(8,128)S(1)}, f32[2,2,256,128]{3,2,1,0:T(8,128)S(1)}, u32[]{:S(2)}, u32[]{:S(2)}) collective-permute-start(f32[2,2,256,128]{3,2,1,0:T(8,128)S(1)} %get-tuple-element.54), channel_id=1, source_target_pairs={{1,2},{9,10},{17,18},{25,26},{3,4},{11,12},{19,20},{27,28},{5,6},{... | collective-permute-start | bytes 1572872 | tf_op jit(solution)/shard_map/ppermute | solution.py:377
  46.6 7.2 %collective-permute-start.16 = (f32[1,128,256]{2,1,0:T(8,128)S(1)}, f32[1,128,256]{2,1,0:T(8,128)S(1)}, u32[]{:S(2)}, u32[]{:S(2)}) collective-permute-start(f32[1,128,256]{2,1,0:T(8,128)S(1)} %get-tuple-element.59), channel_id=1, source_target_pairs={{8,24},{16,0},{9,25},{17,1},{10,26},{18,2},{11,27},{19,3},{12,28},... | collective-permute-start | bytes 393224 | tf_op jit(solution)/shard_map/ppermute | solution.py:403
  50.9 7.9 %collective-permute-start.21 = (f32[2,128,256]{2,1,0:T(8,128)S(1)}, f32[2,128,256]{2,1,0:T(8,128)S(1)}, u32[]{:S(2)}, u32[]{:S(2)}) collective-permute-start(f32[2,128,256]{2,1,0:T(8,128)S(1)} %get-tuple-element.64), channel_id=1, source_target_pairs={{0,8},{1,9},{2,10},{3,11},{4,12},{5,13},{6,14},{7,15},{16,24},{17,... | collective-permute-start | bytes 786440 | tf_op jit(solution)/shard_map/ppermute | solution.py:377
  51.0 14.1 %collective-permute-start.22 = (f32[2,128,256]{2,1,0:T(8,128)S(1)}, f32[2,128,256]{2,1,0:T(8,128)S(1)}, u32[]{:S(2)}, u32[]{:S(2)}) collective-permute-start(f32[2,128,256]{2,1,0:T(8,128)S(1)} %get-tuple-element.65), channel_id=1, source_target_pairs={{8,16},{9,17},{10,18},{11,19},{12,20},{13,21},{14,22},{15,23},{0,1... | collective-permute-start | bytes 786440 | tf_op jit(solution)/shard_map/ppermute | solution.py:377
  53.8 14.1 %collective-permute-start.18 = (f32[2,128,256]{2,1,0:T(8,128)S(1)}, f32[2,128,256]{2,1,0:T(8,128)S(1)}, u32[]{:S(2)}, u32[]{:S(2)}) collective-permute-start(f32[2,128,256]{2,1,0:T(8,128)S(1)} %get-tuple-element.60), channel_id=1, source_target_pairs={{0,8},{1,9},{2,10},{3,11},{4,12},{5,13},{6,14},{7,15},{16,24},{17,... | collective-permute-start | bytes 786440 | tf_op jit(solution)/shard_map/ppermute | solution.py:377
  58.8 14.8 %collective-permute-start.15 = (f32[1,128,256]{2,1,0:T(8,128)S(1)}, f32[1,128,256]{2,1,0:T(8,128)S(1)}, u32[]{:S(2)}, u32[]{:S(2)}) collective-permute-start(f32[1,128,256]{2,1,0:T(8,128)S(1)} %get-tuple-element.58), channel_id=1, source_target_pairs={{8,16},{9,17},{10,18},{11,19},{12,20},{13,21},{14,22},{15,23},{0,1... | collective-permute-start | bytes 393224 | tf_op jit(solution)/shard_map/ppermute | solution.py:377
  65.1 8.4 %collective-permute-start.17 = (f32[1,128,256]{2,1,0:T(8,128)S(1)}, f32[1,128,256]{2,1,0:T(8,128)S(1)}, u32[]{:S(2)}, u32[]{:S(2)}) collective-permute-start(f32[1,128,256]{2,1,0:T(8,128)S(1)} %collective-permute-done.16), channel_id=1, source_target_pairs={{24,16},{0,8},{25,17},{1,9},{26,18},{2,10},{27,19},{3,11},{28,20},... | collective-permute-start | bytes 393224 | tf_op jit(solution)/shard_map/ppermute | solution.py:403
  (6 other events, 51.8 us)

commit v3 on v2

--- a/solution.py
+++ b/solution.py
@@ -358,20 +358,20 @@
     return [at for at in range(count) if at not in paired]
 
 
-def swap(axis, value, odd):
+def swap(axis, value, odd, fill=True):
     rows, cols = lax.axis_size("row"), lax.axis_size("col")
     pairs = []
     if axis == "row":
         for low, high in odd_pairs(rows) if odd else even_pairs(rows):
             pairs += [((low, col), (high, col)) for col in range(cols)]
-        for row in lonely(rows) if odd else ():
+        for row in lonely(rows) if odd and fill else ():
             pairs += [((row, low), (row, high)) for low, high in even_pairs(cols)]
     else:
         for low, high in odd_pairs(cols) if odd else even_pairs(cols):
             pairs += [((row, low), (row, high)) for row in range(rows)]
         step = 2 if rows % 4 == 0 else 1
         across = [row for row in range(rows - step) if row // step % 2 == 0]
-        for col in lonely(cols) if odd else ():
+        for col in lonely(cols) if odd and fill else ():
             pairs += [((row, col), (row + step, col)) for row in across]
     flat = [tuple(row * cols + col for row, col in pair) for pair in pairs]
     return lax.ppermute(value, ("row", "col"), flat + [(b, a) for a, b in flat])
@@ -532,7 +532,7 @@
     direct = swap("row", direct, True)
     rows_o0 = [direct, relay("row", away, 1, False)]
     side_e = swap("col", side_e, False)
-    side_o = swap("col", side_o, True)
+    side_o = swap("col", side_o, True, False)
     whole = shape(*object_tiles.shape)
     outs = ()
     for given, steps in (

time: 74.6 us -> 74.6 us (level)
  waiting for transfers between devices: 23.8 us -> 22.1 us
  starting transfers between devices: 30.3 us -> 31.9 us
    ppermute x19, starting transfers between devices: 22.6 us -> 24.5 us  [swap(): return lax.ppermute(value, ('row', 'col'), flat + [(b, a) for a, b in flat])]
    ppermute x19, waiting for transfers between devices: 19.9 us -> 18.2 us  [swap(): return lax.ppermute(value, ('row', 'col'), flat + [(b, a) for a, b in flat])]
  transfers between devices with their start and end apart: 23 -> 23, of which waited for: 9 -> 8; matrix products, arithmetic and copies ran while one was open for 0% -> 0% of each run, Pallas kernels for 11% -> 11%
where the time goes in v3:
time: 74.6 us; the launch traced here: 74.4 us
  starting transfers between devices  31.9 us (43%)
  waiting for transfers between devices  22.1 us (30%)
  Pallas kernels  17.6 us (24%)
  between operations  1.54 us (2%)
  local copies, waits for them, and re-layouts  1.25 us (2%)
    ppermute x19, starting transfers between devices, swap(): return lax.ppermute(value, ('row', 'col'), flat + [(b, a) for a, b in flat])  24.5 us
    ppermute x19, waiting for transfers between devices, swap(): return lax.ppermute(value, ('row', 'col'), flat + [(b, a) for a, b in flat])  18.2 us
    ppermute x4, starting transfers between devices, relay(): return lax.ppermute(value, axis, steps)  7.47 us
    pallas_call x1, Pallas kernels, per_device(): call(exit_kernel, out_shape=(field, *pieces), in_specs=[VMEM] * 11, out_s...  4.42 us
    ppermute x4, waiting for transfers between devices, relay(): return lax.ppermute(value, axis, steps)  3.86 us
    pallas_call x1, Pallas kernels, per_device(): call(near_kernel, out_shape=field, in_specs=[VMEM] * 11, out_specs=VMEM,...  3.71 us
    pallas_call x1, Pallas kernels, per_device(): call(first_kernel, out_shape=(*pieces[:2], sides, sides, pieces[4]), in_s...  3.71 us
    pallas_call x3, Pallas kernels, per_device(): pl.pallas_call(functools.partial(final_kernel, steps), out_shape=(whole,...  2.86 us
  transfers between devices with their start and end apart: 23, of which 8 were waited for; matrix products, arithmetic and copies ran while one was open for 0% of the time, Pallas kernels for 11%

profile of v3, /device:TPU:11, one launch (start us, length us, event | category | flops | bytes accessed | tf_op | source)
XLA Modules:
  0.0 74.4 jit_solution(5761685587137745206)
XLA Ops:
  0.6 1.2 %copy-done = f32[2,2,256,256]{3,2,1,0:T(8,128)S(1)} copy-done((f32[2,2,256,256]{3,2,1,0:T(8,128)S(1)}, f32[2,2,256,256]{3,2,1,0:T(8,128)}, u32[]{:S(2)}) %copy-start) | copy-done | bytes 1048600
  2.1 1.3 %collective-permute-start.1 = (f32[2,128,256]{2,1,0:T(8,128)S(1)}, f32[2,128,256]{2,1,0:T(8,128)S(1)}, u32[]{:S(2)}, u32[]{:S(2)}) collective-permute-start(f32[2,128,256]{2,1,0:T(8,128)S(1)} %get-tuple-element.38), channel_id=1, source_target_pairs={{8,24},{16,0},{24,8},{0,16},{9,25},{17,1},{25,9},{1,17},{10,26},{1... | collective-permute-start | bytes 786440 | tf_op jit(solution)/shard_map/ppermute | solution.py:403
  3.6 1.2 %collective-permute-start.8 = (f32[2,128,256]{2,1,0:T(8,128)S(1)}, f32[2,128,256]{2,1,0:T(8,128)S(1)}, u32[]{:S(2)}, u32[]{:S(2)}) collective-permute-start(f32[2,128,256]{2,1,0:T(8,128)S(1)} %get-tuple-element.44), channel_id=1, source_target_pairs={{8,16},{9,17},{10,18},{11,19},{12,20},{13,21},{14,22},{15,23},{0,1... | collective-permute-start | bytes 786440 | tf_op jit(solution)/shard_map/ppermute | solution.py:377
  4.8 1.3 %collective-permute-start = (f32[2,128,256]{2,1,0:T(8,128)S(1)}, f32[2,128,256]{2,1,0:T(8,128)S(1)}, u32[]{:S(2)}, u32[]{:S(2)}) collective-permute-start(f32[2,128,256]{2,1,0:T(8,128)S(1)} %get-tuple-element.37), channel_id=1, source_target_pairs={{0,8},{1,9},{2,10},{3,11},{4,12},{5,13},{6,14},{7,15},{16,24},{17,... | collective-permute-start | bytes 786440 | tf_op jit(solution)/shard_map/ppermute | solution.py:377
  6.4 3.0 %collective-permute-done.1 = f32[2,128,256]{2,1,0:T(8,128)S(1)} collective-permute-done((f32[2,128,256]{2,1,0:T(8,128)S(1)}, f32[2,128,256]{2,1,0:T(8,128)S(1)}, u32[]{:S(2)}, u32[]{:S(2)}) %collective-permute-start.1) | collective-permute-done | bytes 262176 | tf_op jit(solution)/shard_map/ppermute | solution.py:403
  9.3 2.9 %collective-permute-start.4 = (f32[2,2,256,128]{3,2,1,0:T(8,128)S(1)}, f32[2,2,256,128]{3,2,1,0:T(8,128)S(1)}, u32[]{:S(2)}, u32[]{:S(2)}) collective-permute-start(f32[2,2,256,128]{3,2,1,0:T(8,128)S(1)} %get-tuple-element.40), channel_id=1, source_target_pairs={{1,2},{9,10},{17,18},{25,26},{3,4},{11,12},{19,20},{27,28},{5,6},{... | collective-permute-start | bytes 1572872 | tf_op jit(solution)/shard_map/ppermute | solution.py:377
  13.3 2.6 %collective-permute-done.8.halo_o.row_o = f32[2,128,256]{2,1,0:T(8,128)S(1)} collective-permute-done((f32[2,128,256]{2,1,0:T(8,128)S(1)}, f32[2,128,256]{2,1,0:T(8,128)S(1)}, u32[]{:S(2)}, u32[]{:S(2)}) %collective-permute-start.8) | collective-permute-done | bytes 262176 | tf_op jit(solution)/shard_map/ppermute | solution.py:377
  15.9 3.3 %collective-permute-start.9 = (f32[2,2,128,128]{3,2,1,0:T(8,128)S(1)}, f32[2,2,128,128]{3,2,1,0:T(8,128)S(1)}, u32[]{:S(2)}, u32[]{:S(2)}) collective-permute-start(f32[2,2,128,128]{3,2,1,0:T(8,128)S(1)} %get-tuple-element.45), channel_id=1, source_target_pairs={{0,1},{8,9},{16,17},{24,25},{2,3},{10,11},{18,19},{26,27},{4,5},{1... | collective-permute-start | bytes 786440 | tf_op jit(solution)/shard_map/ppermute | solution.py:377
  19.6 3.0 %collective-permute-start.10 = (f32[2,2,128,128]{3,2,1,0:T(8,128)S(1)}, f32[2,2,128,128]{3,2,1,0:T(8,128)S(1)}, u32[]{:S(2)}, u32[]{:S(2)}) collective-permute-start(f32[2,2,128,128]{3,2,1,0:T(8,128)S(1)} %get-tuple-element.46), channel_id=1, source_target_pairs={{1,2},{9,10},{17,18},{25,26},{3,4},{11,12},{19,20},{27,28},{5,6},{... | collective-permute-start | bytes 786440 | tf_op jit(solution)/shard_map/ppermute | solution.py:377
  23.4 1.3 %collective-permute-start.6 = (f32[2,2,128,128]{3,2,1,0:T(8,128)S(1)}, f32[2,2,128,128]{3,2,1,0:T(8,128)S(1)}, u32[]{:S(2)}, u32[]{:S(2)}) collective-permute-start(f32[2,2,128,128]{3,2,1,0:T(8,128)S(1)} %get-tuple-element.42), channel_id=1, source_target_pairs={{1,2},{9,10},{17,18},{25,26},{3,4},{11,12},{19,20},{27,28},{5,6},{... | collective-permute-start | bytes 786440 | tf_op jit(solution)/shard_map/ppermute | solution.py:377
  25.4 2.3 %turn.1 = (f32[8,128]{1,0:T(8,128)S(1)}, f32[2,256,256]{2,1,0:T(8,128)S(1)}, bf16[2,3,256,256]{3,2,1,0:T(8,128)(2,1)S(1)}, f32[2,256,256]{2,1,0:T(8,128)S(1)}) custom-call(s32[2,2]{1,0:T(2,128)S(1)} %copy-done.5, s32[1,1]{1,0:T(1,128)S(6)} %copy.17.live, f32[256,256]{1,0:T(8,128)S(1)} %copy-done.4, bf16[2,3,256,256]{3,2,1,0:T(8,128)(2,1)S(1)} %copy-done.2, ...), custom_call_target="tpu_custom_call" | custom-call | tf_op jit(solution)/shard_map/turn/pallas_call | solution.py:454
  27.8 3.7 %near.1 = f32[2,2,256,256]{3,2,1,0:T(8,128)S(1)} custom-call(f32[8,128]{1,0:T(8,128)S(1)} %get-tuple-element.36.slots_at, f32[2,2,256,256]{3,2,1,0:T(8,128)S(1)} %copy-done.1, f32[2,128,256]{2,1,0:T(8,128)S(1)} %collective-permute-done.7.halo_e.row_e, f32[2,128,256]{2,1,0:T(8,128)S(1)} %collective-permute-done.8.halo_o.row_o, ...), custom_call_target="tpu_custom_call" | custom-call | flops 2415919104 | bytes 8388608 | tf_op jit(solution)/shard_map/near/pallas_call | solution.py:477
  31.5 4.4 %exit.1 = (f32[2,2,256,256]{3,2,1,0:T(8,128)S(1)}, f32[2,2,128,128]{3,2,1,0:T(8,128)S(1)}, f32[2,2,128,128]{3,2,1,0:T(8,128)S(1)}, f32[2,256,128]{2,1,0:T(8,128)...) custom-call(f32[8,128]{1,0:T(8,128)S(1)} %get-tuple-element.36.slots_at, f32[2,2,256,256]{3,2,1,0:T(8,128)S(1)} %copy-done.1, ...), custom_call_target="tpu_custom_call" | custom-call | flops 2415919104 | bytes 8388608 | tf_op jit(solution)/shard_map/exit/pallas_call | solution.py:489
  35.9 3.7 %first.1 = (f32[2,2,128,128]{3,2,1,0:T(8,128)S(1)}, f32[2,2,128,128]{3,2,1,0:T(8,128)S(1)}, f32[2,2,256,128]{3,2,1,0:T(8,128)S(1)}, f32[2,2,256,128]{3,2,1,0:T(8,128)S(1)}, f32[2,512,256]{2,1,0:T(8,128)S(1)}) custom-call(f32[8,128]{1,0:T(8,128)S(1)} %get-tuple-element.36.slots_at, f32[2,2,256,256]{3,2,1,0:T(8,128)S(1)} %get-tuple-element.50.g_near, ...), custom_call_target="tpu_custom_call" | custom-call | flops 2415919104 | bytes 8388608 | tf_op jit(solution)/shard_map/first/pallas_call | solution.py:513
  40.4 1.0 %collective-permute-start.14 = (f32[2,2,128,128]{3,2,1,0:T(8,128)S(1)}, f32[2,2,128,128]{3,2,1,0:T(8,128)S(1)}, u32[]{:S(2)}, u32[]{:S(2)}) collective-permute-start(f32[2,2,128,128]{3,2,1,0:T(8,128)S(1)} %get-tuple-element.57), channel_id=1, source_target_pairs={{1,2},{9,10},{17,18},{25,26},{3,4},{11,12},{19,20},{27,28},{5,6},{... | collective-permute-start | bytes 786440 | tf_op jit(solution)/shard_map/ppermute | solution.py:377
  41.4 1.6 %collective-permute-start.19 = (f32[2,2,128,128]{3,2,1,0:T(8,128)S(1)}, f32[2,2,128,128]{3,2,1,0:T(8,128)S(1)}, u32[]{:S(2)}, u32[]{:S(2)}) collective-permute-start(f32[2,2,128,128]{3,2,1,0:T(8,128)S(1)} %get-tuple-element.62), channel_id=1, source_target_pairs={{0,1},{8,9},{16,17},{24,25},{2,3},{10,11},{18,19},{26,27},{4,5},{1... | collective-permute-start | bytes 786440 | tf_op jit(solution)/shard_map/ppermute | solution.py:377
  43.4 3.3 %collective-permute-start.12 = (f32[2,2,256,128]{3,2,1,0:T(8,128)S(1)}, f32[2,2,256,128]{3,2,1,0:T(8,128)S(1)}, u32[]{:S(2)}, u32[]{:S(2)}) collective-permute-start(f32[2,2,256,128]{3,2,1,0:T(8,128)S(1)} %get-tuple-element.54), channel_id=1, source_target_pairs={{1,2},{9,10},{17,18},{25,26},{3,4},{11,12},{19,20},{27,28},{5,6},{... | collective-permute-start | bytes 1572872 | tf_op jit(solution)/shard_map/ppermute | solution.py:377
  46.8 3.9 %collective-permute-start.16 = (f32[1,128,256]{2,1,0:T(8,128)S(1)}, f32[1,128,256]{2,1,0:T(8,128)S(1)}, u32[]{:S(2)}, u32[]{:S(2)}) collective-permute-start(f32[1,128,256]{2,1,0:T(8,128)S(1)} %get-tuple-element.59), channel_id=1, source_target_pairs={{8,24},{16,0},{9,25},{17,1},{10,26},{18,2},{11,27},{19,3},{12,28},... | collective-permute-start | bytes 393224 | tf_op jit(solution)/shard_map/ppermute | solution.py:403
  51.0 1.9 %collective-permute-start.22 = (f32[2,128,256]{2,1,0:T(8,128)S(1)}, f32[2,128,256]{2,1,0:T(8,128)S(1)}, u32[]{:S(2)}, u32[]{:S(2)}) collective-permute-start(f32[2,128,256]{2,1,0:T(8,128)S(1)} %get-tuple-element.65), channel_id=1, source_target_pairs={{8,16},{9,17},{10,18},{11,19},{12,20},{13,21},{14,22},{15,23},{0,1... | collective-permute-start | bytes 786440 | tf_op jit(solution)/shard_map/ppermute | solution.py:377
  54.7 4.0 %collective-permute-done.21.refs_1_ = f32[2,128,256]{2,1,0:T(8,128)S(1)} collective-permute-done((f32[2,128,256]{2,1,0:T(8,128)S(1)}, f32[2,128,256]{2,1,0:T(8,128)S(1)}, u32[]{:S(2)}, u32[]{:S(2)}) %collective-permute-start.21) | collective-permute-done | bytes 262176 | tf_op jit(solution)/shard_map/ppermute | solution.py:377
  59.0 6.1 %collective-permute-done.22.refs_2_ = f32[2,128,256]{2,1,0:T(8,128)S(1)} collective-permute-done((f32[2,128,256]{2,1,0:T(8,128)S(1)}, f32[2,128,256]{2,1,0:T(8,128)S(1)}, u32[]{:S(2)}, u32[]{:S(2)}) %collective-permute-start.22) | collective-permute-done | bytes 262176 | tf_op jit(solution)/shard_map/ppermute | solution.py:377
  65.1 1.3 %collective-permute-start.17 = (f32[1,128,256]{2,1,0:T(8,128)S(1)}, f32[1,128,256]{2,1,0:T(8,128)S(1)}, u32[]{:S(2)}, u32[]{:S(2)}) collective-permute-start(f32[1,128,256]{2,1,0:T(8,128)S(1)} %collective-permute-done.16), channel_id=1, source_target_pairs={{24,16},{0,8},{25,17},{1,9},{26,18},{2,10},{27,19},{3,11},{28,20},... | collective-permute-start | bytes 393224 | tf_op jit(solution)/shard_map/ppermute | solution.py:403
  66.4 1.1 %shard_map.86 = (f32[2,2,256,256]{3,2,1,0:T(8,128)}, f32[2,2,256,256]{3,2,1,0:T(8,128)}) custom-call(f32[2,2,256,256]{3,2,1,0:T(8,128)S(1)} %copy-done.1, f32[2,2,256,128]{3,2,1,0:T(8,128)S(1)} %collective-permute-done.11.side_e, f32[2,2,256,128]{3,2,1,0:T(8,128)S(1)} %collective-permute-done.12.side_o, f32[2,512,256]{2,1,0:T(8,128)S(1)} %get-tuple-element.61.middle.refs_0_, ...), custom_call_target="tpu_custom_call" | custom-call | tf_op jit(solution)/shard_map/pallas_call | solution.py:544
  68.8 4.7 %collective-permute-done.15.refs_1_ = f32[1,128,256]{2,1,0:T(8,128)S(1)} collective-permute-done((f32[1,128,256]{2,1,0:T(8,128)S(1)}, f32[1,128,256]{2,1,0:T(8,128)S(1)}, u32[]{:S(2)}, u32[]{:S(2)}) %collective-permute-start.15) | collective-permute-done | bytes 131104 | tf_op jit(solution)/shard_map/ppermute | solution.py:377
  (48 shorter events, 8.9 us)
Async XLA Ops:
  1.9 23.5 %copy-start.3 = (f32[2,256,256]{2,1,0:T(8,128)S(1)}, f32[2,256,256]{2,1,0:T(8,128)}, u32[]{:S(2)}) copy-start(f32[2,256,256]{2,1,0:T(8,128)} %light.1) | copy-start | bytes 1572868
  2.1 7.3 %collective-permute-start.1 = (f32[2,128,256]{2,1,0:T(8,128)S(1)}, f32[2,128,256]{2,1,0:T(8,128)S(1)}, u32[]{:S(2)}, u32[]{:S(2)}) collective-permute-start(f32[2,128,256]{2,1,0:T(8,128)S(1)} %get-tuple-element.38), channel_id=1, source_target_pairs={{8,24},{16,0},{24,8},{0,16},{9,25},{17,1},{25,9},{1,17},{10,26},{1... | collective-permute-start | bytes 786440 | tf_op jit(solution)/shard_map/ppermute | solution.py:403
  3.4 8.9 %collective-permute-start.7 = (f32[2,128,256]{2,1,0:T(8,128)S(1)}, f32[2,128,256]{2,1,0:T(8,128)S(1)}, u32[]{:S(2)}, u32[]{:S(2)}) collective-permute-start(f32[2,128,256]{2,1,0:T(8,128)S(1)} %get-tuple-element.43), channel_id=1, source_target_pairs={{0,8},{1,9},{2,10},{3,11},{4,12},{5,13},{6,14},{7,15},{16,24},{17,... | collective-permute-start | bytes 786440 | tf_op jit(solution)/shard_map/ppermute | solution.py:377
  3.6 12.2 %collective-permute-start.8 = (f32[2,128,256]{2,1,0:T(8,128)S(1)}, f32[2,128,256]{2,1,0:T(8,128)S(1)}, u32[]{:S(2)}, u32[]{:S(2)}) collective-permute-start(f32[2,128,256]{2,1,0:T(8,128)S(1)} %get-tuple-element.44), channel_id=1, source_target_pairs={{8,16},{9,17},{10,18},{11,19},{12,20},{13,21},{14,22},{15,23},{0,1... | collective-permute-start | bytes 786440 | tf_op jit(solution)/shard_map/ppermute | solution.py:377
  4.8 14.8 %collective-permute-start = (f32[2,128,256]{2,1,0:T(8,128)S(1)}, f32[2,128,256]{2,1,0:T(8,128)S(1)}, u32[]{:S(2)}, u32[]{:S(2)}) collective-permute-start(f32[2,128,256]{2,1,0:T(8,128)S(1)} %get-tuple-element.37), channel_id=1, source_target_pairs={{0,8},{1,9},{2,10},{3,11},{4,12},{5,13},{6,14},{7,15},{16,24},{17,... | collective-permute-start | bytes 786440 | tf_op jit(solution)/shard_map/ppermute | solution.py:377
  6.1 21.6 %collective-permute-start.3 = (f32[2,2,256,128]{3,2,1,0:T(8,128)S(1)}, f32[2,2,256,128]{3,2,1,0:T(8,128)S(1)}, u32[]{:S(2)}, u32[]{:S(2)}) collective-permute-start(f32[2,2,256,128]{3,2,1,0:T(8,128)S(1)} %get-tuple-element.39), channel_id=1, source_target_pairs={{0,1},{8,9},{16,17},{24,25},{2,3},{10,11},{18,19},{26,27},{4,5},{1... | collective-permute-start | bytes 1572872 | tf_op jit(solution)/shard_map/ppermute | solution.py:377
  9.3 18.4 %collective-permute-start.4 = (f32[2,2,256,128]{3,2,1,0:T(8,128)S(1)}, f32[2,2,256,128]{3,2,1,0:T(8,128)S(1)}, u32[]{:S(2)}, u32[]{:S(2)}) collective-permute-start(f32[2,2,256,128]{3,2,1,0:T(8,128)S(1)} %get-tuple-element.40), channel_id=1, source_target_pairs={{1,2},{9,10},{17,18},{25,26},{3,4},{11,12},{19,20},{27,28},{5,6},{... | collective-permute-start | bytes 1572872 | tf_op jit(solution)/shard_map/ppermute | solution.py:377
  12.3 10.3 %collective-permute-start.2 = (f32[2,128,256]{2,1,0:T(8,128)S(1)}, f32[2,128,256]{2,1,0:T(8,128)S(1)}, u32[]{:S(2)}, u32[]{:S(2)}) collective-permute-start(f32[2,128,256]{2,1,0:T(8,128)S(1)} %collective-permute-done.1), channel_id=1, source_target_pairs={{24,16},{0,8},{8,24},{16,0},{25,17},{1,9},{9,25},{17,1},{26,18},{2... | collective-permute-start | bytes 786440 | tf_op jit(solution)/shard_map/ppermute | solution.py:403
  15.9 7.6 %collective-permute-start.9 = (f32[2,2,128,128]{3,2,1,0:T(8,128)S(1)}, f32[2,2,128,128]{3,2,1,0:T(8,128)S(1)}, u32[]{:S(2)}, u32[]{:S(2)}) collective-permute-start(f32[2,2,128,128]{3,2,1,0:T(8,128)S(1)} %get-tuple-element.45), channel_id=1, source_target_pairs={{0,1},{8,9},{16,17},{24,25},{2,3},{10,11},{18,19},{26,27},{4,5},{1... | collective-permute-start | bytes 786440 | tf_op jit(solution)/shard_map/ppermute | solution.py:377
  19.6 8.1 %collective-permute-start.10 = (f32[2,2,128,128]{3,2,1,0:T(8,128)S(1)}, f32[2,2,128,128]{3,2,1,0:T(8,128)S(1)}, u32[]{:S(2)}, u32[]{:S(2)}) collective-permute-start(f32[2,2,128,128]{3,2,1,0:T(8,128)S(1)} %get-tuple-element.46), channel_id=1, source_target_pairs={{1,2},{9,10},{17,18},{25,26},{3,4},{11,12},{19,20},{27,28},{5,6},{... | collective-permute-start | bytes 786440 | tf_op jit(solution)/shard_map/ppermute | solution.py:377
  22.6 8.9 %collective-permute-start.5 = (f32[2,2,128,128]{3,2,1,0:T(8,128)S(1)}, f32[2,2,128,128]{3,2,1,0:T(8,128)S(1)}, u32[]{:S(2)}, u32[]{:S(2)}) collective-permute-start(f32[2,2,128,128]{3,2,1,0:T(8,128)S(1)} %get-tuple-element.41), channel_id=1, source_target_pairs={{0,1},{8,9},{16,17},{24,25},{2,3},{10,11},{18,19},{26,27},{4,5},{1... | collective-permute-start | bytes 786440 | tf_op jit(solution)/shard_map/ppermute | solution.py:377
  23.4 8.0 %collective-permute-start.6 = (f32[2,2,128,128]{3,2,1,0:T(8,128)S(1)}, f32[2,2,128,128]{3,2,1,0:T(8,128)S(1)}, u32[]{:S(2)}, u32[]{:S(2)}) collective-permute-start(f32[2,2,128,128]{3,2,1,0:T(8,128)S(1)} %get-tuple-element.42), channel_id=1, source_target_pairs={{1,2},{9,10},{17,18},{25,26},{3,4},{11,12},{19,20},{27,28},{5,6},{... | collective-permute-start | bytes 786440 | tf_op jit(solution)/shard_map/ppermute | solution.py:377
  39.6 3.7 %collective-permute-start.13 = (f32[2,2,128,128]{3,2,1,0:T(8,128)S(1)}, f32[2,2,128,128]{3,2,1,0:T(8,128)S(1)}, u32[]{:S(2)}, u32[]{:S(2)}) collective-permute-start(f32[2,2,128,128]{3,2,1,0:T(8,128)S(1)} %get-tuple-element.56), channel_id=1, source_target_pairs={{0,1},{8,9},{16,17},{24,25},{2,3},{10,11},{18,19},{26,27},{4,5},{1... | collective-permute-start | bytes 786440 | tf_op jit(solution)/shard_map/ppermute | solution.py:377
  40.4 6.3 %collective-permute-start.14 = (f32[2,2,128,128]{3,2,1,0:T(8,128)S(1)}, f32[2,2,128,128]{3,2,1,0:T(8,128)S(1)}, u32[]{:S(2)}, u32[]{:S(2)}) collective-permute-start(f32[2,2,128,128]{3,2,1,0:T(8,128)S(1)} %get-tuple-element.57), channel_id=1, source_target_pairs={{1,2},{9,10},{17,18},{25,26},{3,4},{11,12},{19,20},{27,28},{5,6},{... | collective-permute-start | bytes 786440 | tf_op jit(solution)/shard_map/ppermute | solution.py:377
  41.4 9.3 %collective-permute-start.19 = (f32[2,2,128,128]{3,2,1,0:T(8,128)S(1)}, f32[2,2,128,128]{3,2,1,0:T(8,128)S(1)}, u32[]{:S(2)}, u32[]{:S(2)}) collective-permute-start(f32[2,2,128,128]{3,2,1,0:T(8,128)S(1)} %get-tuple-element.62), channel_id=1, source_target_pairs={{0,1},{8,9},{16,17},{24,25},{2,3},{10,11},{18,19},{26,27},{4,5},{1... | collective-permute-start | bytes 786440 | tf_op jit(solution)/shard_map/ppermute | solution.py:377
  43.0 7.8 %collective-permute-start.20 = (f32[2,2,128,128]{3,2,1,0:T(8,128)S(1)}, f32[2,2,128,128]{3,2,1,0:T(8,128)S(1)}, u32[]{:S(2)}, u32[]{:S(2)}) collective-permute-start(f32[2,2,128,128]{3,2,1,0:T(8,128)S(1)} %get-tuple-element.63), channel_id=1, source_target_pairs={{1,2},{9,10},{17,18},{25,26},{3,4},{11,12},{19,20},{27,28},{5,6},{... | collective-permute-start | bytes 786440 | tf_op jit(solution)/shard_map/ppermute | solution.py:377
  43.0 23.4 %collective-permute-start.11 = (f32[2,2,256,128]{3,2,1,0:T(8,128)S(1)}, f32[2,2,256,128]{3,2,1,0:T(8,128)S(1)}, u32[]{:S(2)}, u32[]{:S(2)}) collective-permute-start(f32[2,2,256,128]{3,2,1,0:T(8,128)S(1)} %get-tuple-element.53), channel_id=1, source_target_pairs={{0,1},{8,9},{16,17},{24,25},{2,3},{10,11},{18,19},{26,27},{4,5},{1... | collective-permute-start | bytes 1572872 | tf_op jit(solution)/shard_map/ppermute | solution.py:377
  43.4 23.0 %collective-permute-start.12 = (f32[2,2,256,128]{3,2,1,0:T(8,128)S(1)}, f32[2,2,256,128]{3,2,1,0:T(8,128)S(1)}, u32[]{:S(2)}, u32[]{:S(2)}) collective-permute-start(f32[2,2,256,128]{3,2,1,0:T(8,128)S(1)} %get-tuple-element.54), channel_id=1, source_target_pairs={{1,2},{9,10},{17,18},{25,26},{3,4},{11,12},{19,20},{27,28},{5,6},{... | collective-permute-start | bytes 1572872 | tf_op jit(solution)/shard_map/ppermute | solution.py:377
  46.8 6.9 %collective-permute-start.16 = (f32[1,128,256]{2,1,0:T(8,128)S(1)}, f32[1,128,256]{2,1,0:T(8,128)S(1)}, u32[]{:S(2)}, u32[]{:S(2)}) collective-permute-start(f32[1,128,256]{2,1,0:T(8,128)S(1)} %get-tuple-element.59), channel_id=1, source_target_pairs={{8,24},{16,0},{9,25},{17,1},{10,26},{18,2},{11,27},{19,3},{12,28},... | collective-permute-start | bytes 393224 | tf_op jit(solution)/shard_map/ppermute | solution.py:403
  50.9 7.9 %collective-permute-start.21 = (f32[2,128,256]{2,1,0:T(8,128)S(1)}, f32[2,128,256]{2,1,0:T(8,128)S(1)}, u32[]{:S(2)}, u32[]{:S(2)}) collective-permute-start(f32[2,128,256]{2,1,0:T(8,128)S(1)} %get-tuple-element.64), channel_id=1, source_target_pairs={{0,8},{1,9},{2,10},{3,11},{4,12},{5,13},{6,14},{7,15},{16,24},{17,... | collective-permute-start | bytes 786440 | tf_op jit(solution)/shard_map/ppermute | solution.py:377
  51.0 14.1 %collective-permute-start.22 = (f32[2,128,256]{2,1,0:T(8,128)S(1)}, f32[2,128,256]{2,1,0:T(8,128)S(1)}, u32[]{:S(2)}, u32[]{:S(2)}) collective-permute-start(f32[2,128,256]{2,1,0:T(8,128)S(1)} %get-tuple-element.65), channel_id=1, source_target_pairs={{8,16},{9,17},{10,18},{11,19},{12,20},{13,21},{14,22},{15,23},{0,1... | collective-permute-start | bytes 786440 | tf_op jit(solution)/shard_map/ppermute | solution.py:377
  53.8 14.1 %collective-permute-start.18 = (f32[2,128,256]{2,1,0:T(8,128)S(1)}, f32[2,128,256]{2,1,0:T(8,128)S(1)}, u32[]{:S(2)}, u32[]{:S(2)}) collective-permute-start(f32[2,128,256]{2,1,0:T(8,128)S(1)} %get-tuple-element.60), channel_id=1, source_target_pairs={{0,8},{1,9},{2,10},{3,11},{4,12},{5,13},{6,14},{7,15},{16,24},{17,... | collective-permute-start | bytes 786440 | tf_op jit(solution)/shard_map/ppermute | solution.py:377
  58.8 14.8 %collective-permute-start.15 = (f32[1,128,256]{2,1,0:T(8,128)S(1)}, f32[1,128,256]{2,1,0:T(8,128)S(1)}, u32[]{:S(2)}, u32[]{:S(2)}) collective-permute-start(f32[1,128,256]{2,1,0:T(8,128)S(1)} %get-tuple-element.58), channel_id=1, source_target_pairs={{8,16},{9,17},{10,18},{11,19},{12,20},{13,21},{14,22},{15,23},{0,1... | collective-permute-start | bytes 393224 | tf_op jit(solution)/shard_map/ppermute | solution.py:377
  65.1 8.4 %collective-permute-start.17 = (f32[1,128,256]{2,1,0:T(8,128)S(1)}, f32[1,128,256]{2,1,0:T(8,128)S(1)}, u32[]{:S(2)}, u32[]{:S(2)}) collective-permute-start(f32[1,128,256]{2,1,0:T(8,128)S(1)} %collective-permute-done.16), channel_id=1, source_target_pairs={{24,16},{0,8},{25,17},{1,9},{26,18},{2,10},{27,19},{3,11},{28,20},... | collective-permute-start | bytes 393224 | tf_op jit(solution)/shard_map/ppermute | solution.py:403
  (6 other events, 51.8 us)
